TPU v7x, 32 devices: a 4x4x1 block of a 4x4x8 slice. The times are simulated.
32 devices in a mesh: dp: 1 (over z), col: 4 (over y), row: 8 (over x, core).
Axes of the slice: x: 4, y: 4, z: 1, core: 2. Of those that a mesh axis runs over, the one named last changes fastest.
The devices are a block of a 4x4x8 slice.
Arguments:
- x_in: bfloat16 [2, 2048, 4096], P(None, ('dp', 'row'), 'col')
- ln_gamma: float32 [4096], P('col')
- w_in: bfloat16 [4096, 16384], P('row', 'col')
- w_out: bfloat16 [16384, 4096], P('row', 'col')
Outputs:
- output: bfloat16 [2, 2048, 4096], P(None, ('dp', 'row'), 'col')
All inputs are finite; a program needn't handle non-finite values.
Results may differ from a plain program's by a relative error of at most 0.001.
Values are sent between devices in bfloat16 or wider.
A program may use at most 768 MiB of HBM per device.

v0:
```python
import jax
import jax.numpy as jnp
from jax import lax
from jax.sharding import PartitionSpec as P

LN_EPS = 1e-5


def solution(mesh):
    col_size = mesh.shape["col"]
    act_spec = P(None, ("dp", "row"), "col")

    def per_device(x_blk, gamma_blk, w_in_blk, w_out_blk):
        d_model = gamma_blk.shape[0] * col_size
        x_f32 = x_blk.astype(jnp.float32)
        row_stats = jnp.stack([jnp.sum(x_f32, axis=-1), jnp.sum(x_f32 * x_f32, axis=-1)])
        row_stats = lax.psum(row_stats, "col")
        row_mean = row_stats[0] / d_model
        row_var = row_stats[1] / d_model - row_mean * row_mean
        inv_std = lax.rsqrt(row_var + LN_EPS)
        z_norm = ((x_f32 - row_mean[..., None]) * inv_std[..., None] * gamma_blk).astype(jnp.bfloat16)
        z_panel = lax.all_gather(z_norm, "col", axis=2, tiled=True)
        w_in_panel = lax.all_gather(w_in_blk, "row", axis=0, tiled=True)
        hidden = jnp.dot(z_panel, w_in_panel, preferred_element_type=jnp.float32)
        hidden = jax.nn.gelu(hidden, approximate=True).astype(jnp.bfloat16)
        h_panel = lax.all_gather(hidden, "col", axis=2, tiled=True)
        w_out_panel = lax.all_gather(w_out_blk, "row", axis=0, tiled=True)
        branch = jnp.dot(h_panel, w_out_panel, preferred_element_type=jnp.float32)
        return (x_f32 + branch).astype(jnp.bfloat16)

    return jax.shard_map(per_device, mesh=mesh, in_specs=(act_spec, P("col"), P("row", "col"), P("row", "col")), out_specs=act_spec, check_vma=False)
```

profile of v0, /device:TPU:97, one launch (start us, length us, event | category | flops | bytes accessed | tf_op | source)
XLA Modules:
  0.0 568.6 jit_solution(6042369551894548202)
XLA Ops:
  6.5 0.0 all-gather.5.cloned.1.call-start
  6.6 1.6 convert_reduce_fusion
  8.2 11.2 %psum.7 = f32[2,2,256]{2,1,0:T(2,128)S(1)} all-reduce(f32[2,2,256]{2,1,0:T(2,128)S(1)} %pad_maximum_fusion), channel_id=1, replica_groups=mesh['dp'=1,'col'=4,'row'=8] {'col'}, use_global_device_ids=true, to_apply=%region_2.0 | all-reduce | flops 1024 | bytes 8192 | tf_op jit(solution)/shard_map/psum | solution.py:17
  19.4 2.6 fusion.17
  22.0 0.1 all-gather.5.cloned.1.call-update
  22.1 0.1 all-gather.7.cloned.1.call-start
  22.1 0.7 all-gather.7.cloned.1.call-update
  22.9 0.1 all-gather.11.cloned.1.call-start
  23.0 0.7 all-gather.11.cloned.1.call-update
  23.7 0.0 copy-start
  23.7 0.1 all-gather.9.cloned.1.call-start
  23.8 45.1 %all-gather.5.cloned.1.call-done = bf16[2,256,4096]{2,1,0:T(8,128)(2,1)} async-done(((bf16[2,256,1024]{2,1,0:T(8,128)(2,1)}), bf16[2,256,4096]{2,1,0:T(8,128)(2,1)}) %all-gather.5.cloned.1.call-update) | async-done | bytes 4194320 | tf_op jit(solution)/shard_map/all_gather | solution.py:22
  68.9 156.9 %all-gather.7.cloned.1.call-done = bf16[4096,4096]{1,0:T(8,128)(2,1)} async-done(((bf16[512,4096]{1,0:T(8,128)(2,1)}), bf16[4096,4096]{1,0:T(8,128)(2,1)}) %all-gather.7.cloned.1.call-update) | async-done | bytes 33554448 | tf_op jit(solution)/shard_map/all_gather | solution.py:23
  225.7 25.3 %fusion.11 = bf16[2,256,4096]{2,1,0:T(8,128)(2,1)} fusion(bf16[2,256,4096]{2,1,0:T(8,128)(2,1)} %all-gather.5.cloned.1.call-done, bf16[4096,4096]{1,0:T(8,128)(2,1)} %all-gather.7.cloned.1.call-done), kind=kOutput, calls=%fused_computation.12 | convolution fusion | flops 17198743552 | bytes 41943040 | tf_op jit(solution)/shard_map/dot_general | solution.py:24
  251.0 0.1 all-gather.9.cloned.1.call-update
  251.1 131.5 %all-gather.11.cloned.1.call-done = bf16[16384,1024]{1,0:T(8,128)(2,1)} async-done(((bf16[2048,1024]{1,0:T(8,128)(2,1)}), bf16[16384,1024]{1,0:T(8,128)(2,1)}) %all-gather.11.cloned.1.call-update) | async-done | bytes 33554448 | tf_op jit(solution)/shard_map/all_gather | solution.py:27
  382.5 154.1 %all-gather.9.cloned.1.call-done = bf16[2,256,16384]{2,1,0:T(8,128)(2,1)} async-done(((bf16[2,256,4096]{2,1,0:T(8,128)(2,1)}), bf16[2,256,16384]{2,1,0:T(8,128)(2,1)}) %all-gather.9.cloned.1.call-update) | async-done | bytes 16777232 | tf_op jit(solution)/shard_map/all_gather | solution.py:26
  536.6 0.0 copy-done
  536.6 25.4 %fusion.18 = bf16[2,256,1024]{2,1,0:T(8,128)(2,1)} fusion(bf16[2,256,1024]{2,1,0:T(8,128)(2,1)S(1)} %copy-done, bf16[2,256,16384]{2,1,0:T(8,128)(2,1)} %all-gather.9.cloned.1.call-done, bf16[16384,1024]{1,0:T(8,128)(2,1)} %all-gather.11.cloned.1.call-done), kind=kOutput, calls=%fused_computation.21 | convolution fusion | flops 17181442048 | bytes 52428800 | tf_op jit(solution)/shard_map/dot_general | solution.py:28
  (3 shorter events, 0.0 us)
Async XLA Ops:
  6.5 62.3 %all-gather.5.cloned.1.call-start = ((), (), s32[]{:S(2)}) async-start(), calls=%async_computation | async-start | bytes 5242880 | tf_op jit(solution)/shard_map/all_gather | solution.py:22
  22.1 203.7 %all-gather.7.cloned.1.call-start = ((), (), s32[]{:S(2)}) async-start(), calls=%async_computation.1 | async-start | bytes 37748736 | tf_op jit(solution)/shard_map/all_gather | solution.py:23
  22.9 359.6 %all-gather.11.cloned.1.call-start = ((), (), s32[]{:S(2)}) async-start(), calls=%async_computation.3 | async-start | bytes 37748736 | tf_op jit(solution)/shard_map/all_gather | solution.py:27
  23.7 512.9 %copy-start = (bf16[2,256,1024]{2,1,0:T(8,128)(2,1)S(1)}, bf16[2,256,1024]{2,1,0:T(8,128)(2,1)}, u32[]{:S(2)}) copy-start(bf16[2,256,1024]{2,1,0:T(8,128)(2,1)} %param.4) | copy-start | bytes 3145732
  23.7 512.9 %all-gather.9.cloned.1.call-start = ((), (), s32[]{:S(2)}) async-start(), calls=%async_computation.2 | async-start | bytes 20971520 | tf_op jit(solution)/shard_map/all_gather | solution.py:26
Sparse Core Ops, SparseCore 0:
  22.2 46.6 all-gather.4
  70.5 155.1 all-gather.6
  227.4 155.1 all-gather.10
  383.9 152.6 all-gather.8
where the time goes:
time: 569 us
  waiting for transfers between devices  489 us (86%)
  matrix products  50.7 us (9%)
  between operations  13.2 us (2%)
  blocking collectives  11.2 us (2%)
    all_gather x1, waiting for transfers between devices, per_device(): w_in_panel = lax.all_gather(w_in_blk, 'row', axis=0, tiled=True)  157 us
    all_gather x1, waiting for transfers between devices, per_device(): h_panel = lax.all_gather(hidden, 'col', axis=2, tiled=True)  154 us
    all_gather x1, waiting for transfers between devices, per_device(): w_out_panel = lax.all_gather(w_out_blk, 'row', axis=0, tiled=True)  131 us
    all_gather x1, waiting for transfers between devices, per_device(): z_panel = lax.all_gather(z_norm, 'col', axis=2, tiled=True)  45.1 us
    dot_general x1, matrix products, per_device(): branch = jnp.dot(h_panel, w_out_panel, preferred_element_type=jnp.float32)  25.4 us
    dot_general x1, matrix products, per_device(): hidden = jnp.dot(z_panel, w_in_panel, preferred_element_type=jnp.float32)  25.3 us
  transfers between devices with their start and end apart: 4, of which 4 were waited for; matrix products, arithmetic and copies ran while one was open for 4% of the time, Pallas kernels for 0%

commit v1 on v0

v1 whole, which is shorter than its diff:
```python
import functools

import jax
import jax.numpy as jnp
from jax import lax
from jax.experimental import pallas as pl
from jax.experimental.pallas import tpu as pltpu
from jax.sharding import PartitionSpec as P

LN_EPS = 1e-5
MESH = pl.DeviceIdType.MESH
CHUNKS = 4
N_SEMS = 144
GELU_C = 0.7978845608028654


class Comm:
    def __init__(self, send_sems, recv_sems, some_peer):
        self.send_sems, self.recv_sems, self.some_peer = send_sems, recv_sems, some_peer
        self.ids, self.sent = {}, []

    def _id(self, key):
        return self.ids.setdefault(key, len(self.ids))

    def send(self, key, src, dst, dev):
        i = self._id(key)
        copy = pltpu.make_async_remote_copy(
            src_ref=src, dst_ref=dst, send_sem=self.send_sems.at[i], recv_sem=self.recv_sems.at[i], device_id=dev, device_id_type=MESH
        )
        copy.start()
        self.sent.append(copy)

    def arrive(self, key, ref):
        i = self._id(key)
        pltpu.make_async_remote_copy(
            src_ref=ref, dst_ref=ref, send_sem=self.send_sems.at[i], recv_sem=self.recv_sems.at[i], device_id=self.some_peer, device_id_type=MESH
        ).wait_recv()

    def finish(self):
        for copy in self.sent:
            copy.wait_send()


def kernel(nx, ny, x_ref, gamma_ref, w1_ref, w2_ref, out_ref, xland, zb, w1b, w2b, hb, y0, yr, y1, gb, send_sems, recv_sems, loc_sems):
    T, D = x_ref.shape
    KR, FL = w1_ref.shape
    R2, N = w2_ref.shape
    FH = FL // 2
    FC = FH // CHUNKS
    NC = N // CHUNKS
    T2 = T // 2
    RH = R2 // 2

    row, y = lax.axis_index("row"), lax.axis_index("col")
    x, c = row // 2, row % 2
    xp, xi = nx - 1 - x, x + 1 - 2 * (x % 2)
    xf = nx - 1 - xi
    g = x // (nx // 2)
    up, dn, far = (y + 1) % ny, (y + ny - 1) % ny, (y + 2) % ny
    PX, PI, PC = {"row": 2 * xp + c}, {"row": 2 * xi + c}, {"row": 2 * x + 1 - c}
    YP, YM, YF = {"col": up}, {"col": dn}, {"col": far}

    barrier = pltpu.get_barrier_semaphore()
    for peer in (PX, PI, PC, YP, YM, YF):
        pl.semaphore_signal(barrier, inc=1, device_id=peer, device_id_type=MESH)
    pl.semaphore_wait(barrier, 6)

    comm = Comm(send_sems, recv_sems, PC)
    local = {}

    def local_copy(key, src, dst):
        copy = pltpu.make_async_copy(src, dst, loc_sems.at[len(local)])
        copy.start()
        local[key] = copy

    def tok(half):
        return pl.ds(half * T2, T2)

    def w1_src(grp, j):
        q, s = j // 2, j % 2
        col = pl.multiple_of(q * R2 + grp * RH + s * FC, FC)
        return w1_ref.at[:, pl.ds(col, FC)]

    def w1_dst(j, xx, cc):
        return w1b.at[j, pl.ds(pl.multiple_of((2 * xx + cc) * KR, KR), KR), :]

    def w2_src(grp, n):
        return w2_ref.at[pl.ds(pl.multiple_of(grp * RH, RH), RH), pl.ds(n * NC, NC)]

    def w2_dst(n, xx, cc):
        return w2b.at[n, pl.ds(pl.multiple_of((2 * xx + cc) * RH, RH), RH), :]

    def xl(h, yy, half):
        return xland.at[h, yy, tok(half), :]

    def hs(k, yy, half):
        h, j = divmod(k, CHUNKS)
        return hb.at[h, yy, tok(half), pl.ds(j * FC, FC)]

    for half in (0, 1):
        comm.send(("xp", half), x_ref.at[tok(half), :], xl(0, y, half), PX)
    for a, b in ((0, 1), (1, 0)):
        comm.send(("x1P", a), x_ref.at[tok(a), :], xl(1, y, a), YP)
        comm.send(("x1M", b), x_ref.at[tok(b), :], xl(1, y, b), YM)
    for j in range(CHUNKS):
        comm.send(("w1x", j), w1_src(1 - g, j), w1_dst(j, x, c), PX)
        comm.send(("w1i", j), w1_src(g, j), w1_dst(j, x, c), PI)
        comm.send(("w1c", 0, j), w1_src(g, j), w1_dst(j, x, c), PC)
        local_copy(("w1", j), w1_src(g, j), w1_dst(j, x, c))
    for yk, dev in (("P", YP), ("M", YM), ("F", YF)):
        comm.send(("g" + yk,), gamma_ref, gb.at[y], dev)
    local_copy("g", gamma_ref, gb.at[y])
    for n in range(CHUNKS):
        comm.send(("w2x", n), w2_src(1 - g, n), w2_dst(n, x, c), PX)
        comm.send(("w2c", 0, n), w2_src(g, n), w2_dst(n, x, c), PC)
        local_copy(("w2", n), w2_src(g, n), w2_dst(n, x, c))

    def w_from_inner(w, dst, j):
        comm.arrive((w + "i", j), dst(j, xi, c))
        comm.send((w + "c", 1, j), dst(j, xi, c), dst(j, xi, c), PC)

    def w_from_pair(w, dst, j):
        comm.arrive((w + "x", j), dst(j, xp, c))
        comm.send((w + "f", j), dst(j, xp, c), dst(j, xp, c), PI)
        comm.send((w + "c", 2, j), dst(j, xp, c), dst(j, xp, c), PC)

    def w_from_far(w, dst, j):
        comm.arrive((w + "f", j), dst(j, xf, c))
        comm.send((w + "c", 3, j), dst(j, xf, c), dst(j, xf, c), PC)

    def w_ready(w, dst, j):
        for i, xx in enumerate((x, xi, xp, xf)):
            comm.arrive((w + "c", i, j), dst(j, xx, 1 - c))
        local[(w, j)].wait()

    def x_load(h):
        if h == 0:
            local_copy(("z", h, 0), xland.at[0, y], zb.at[y])
        else:
            local_copy(("z", h, 0), x_ref, zb.at[y])
        for i, yy in enumerate((up, dn, far)):
            local_copy(("z", h, i + 1), xland.at[h, yy], zb.at[yy])
        for i in range(4):
            local[("z", h, i)].wait()

    def norm():
        rb = 32

        def body(i, carry):
            rows = pl.ds(pl.multiple_of(i * rb, rb), rb)
            s = jnp.zeros((rb, 1), jnp.float32)
            q = jnp.zeros((rb, 1), jnp.float32)
            for yy in range(ny):
                v = zb[yy, rows, :].astype(jnp.float32)
                s += jnp.sum(v, axis=-1, keepdims=True)
                q += jnp.sum(v * v, axis=-1, keepdims=True)
            mu = s / (ny * D)
            var = q / (ny * D) - mu * mu
            inv = lax.rsqrt(var + LN_EPS)
            for yy in range(ny):
                v = zb[yy, rows, :].astype(jnp.float32)
                zb[yy, rows, :] = ((v - mu) * inv * gb[yy]).astype(jnp.bfloat16)
            return carry

        lax.fori_loop(0, T // rb, body, 0)

    def hidden(k):
        h, j = divmod(k, CHUNKS)
        mb = T2

        def body(i, carry):
            rows = pl.ds(pl.multiple_of(i * mb, mb), mb)
            u = jnp.zeros((mb, FC), jnp.float32)
            for yy in range(ny):
                u += jnp.dot(zb[yy, rows, :], w1b[j, yy * D : (yy + 1) * D, :], preferred_element_type=jnp.float32)
            cdf = 0.5 * (1.0 + jnp.tanh(GELU_C * (u + 0.044715 * (u * u * u))))
            hb[h, y, rows, j * FC : (j + 1) * FC] = (u * cdf).astype(jnp.bfloat16)
            return carry

        lax.fori_loop(0, T // mb, body, 0)
        for a, b in ((0, 1), (1, 0)):
            comm.send(("hP", k, a), hs(k, y, a), hs(k, y, a), YP)
            comm.send(("hM", k, b), hs(k, y, b), hs(k, y, b), YM)

    def relay(k):
        comm.arrive(("hP", k, 0), hs(k, dn, 0))
        comm.send(("fP", k), hs(k, dn, 0), hs(k, dn, 0), YP)
        comm.arrive(("hM", k, 1), hs(k, up, 1))
        comm.send(("fM", k), hs(k, up, 1), hs(k, up, 1), YM)

    def h_ready(k):
        comm.arrive(("hP", k, 1), hs(k, dn, 1))
        comm.arrive(("hM", k, 0), hs(k, up, 0))

    def far_ready(k):
        comm.arrive(("fP", k), hs(k, far, 0))
        comm.arrive(("fM", k), hs(k, far, 1))

    def project(h, acc, n, yys, j0, j1, first):
        for yy in yys:
            lo, size = j0 * FC, (j1 - j0) * FC
            base = yy * FH + lo
            if not isinstance(base, int):
                base = pl.multiple_of(base, FC)
            d = jnp.dot(hb[h, yy, :, lo : lo + size], w2b[n, pl.ds(base, size), :], preferred_element_type=jnp.float32)
            if first:
                acc[n] = d
                first = False
            else:
                acc[n] += d

    def partial_out(n):
        w_ready("w2", w2_dst, n)
        project(0, y0, n, range(ny), 0, CHUNKS, True)
        comm.send(("y", n), y0.at[n], yr.at[n], PX)

    comm.arrive(("xp", 0), xl(0, y, 0))
    comm.send(("x0P", 0), xl(0, y, 0), xl(0, y, 0), YP)
    comm.arrive(("xp", 1), xl(0, y, 1))
    comm.send(("x0P", 1), xl(0, y, 1), xl(0, y, 1), YP)
    comm.send(("x0M", 1), xl(0, y, 1), xl(0, y, 1), YM)
    comm.send(("x0M", 0), xl(0, y, 0), xl(0, y, 0), YM)
    w_from_inner("w1", w1_dst, 0)
    for h in (0, 1):
        hk = "x%d" % h
        comm.arrive((hk + "P", 0), xl(h, dn, 0))
        comm.send((hk + "p",), xl(h, dn, 0), xl(h, dn, 0), YP)
        comm.arrive((hk + "M", 1), xl(h, up, 1))
        comm.send((hk + "m",), xl(h, up, 1), xl(h, up, 1), YM)
        w_from_pair("w1", w1_dst, h)
        w_from_inner("w1", w1_dst, h + 1)
    w_from_inner("w1", w1_dst, 3)
    w_from_pair("w1", w1_dst, 2)

    def x_ready(h):
        hk = "x%d" % h
        comm.arrive((hk + "P", 1), xl(h, dn, 1))
        comm.arrive((hk + "M", 0), xl(h, up, 0))
        comm.arrive((hk + "p",), xl(h, far, 0))
        comm.arrive((hk + "m",), xl(h, far, 1))

    local["g"].wait()
    for yk, yy in (("P", dn), ("M", up), ("F", far)):
        comm.arrive(("g" + yk,), gb.at[yy])
    x_ready(0)
    x_load(0)
    norm()

    def w2_inner(n):
        comm.send(("w2i", n), w2_src(g, n), w2_dst(n, x, c), PI)

    w_from_far("w1", w1_dst, 0)
    w_ready("w1", w1_dst, 0)
    hidden(0)
    w_from_pair("w1", w1_dst, 3)
    w2_inner(0)
    for k in (1, 2, 3):
        w_from_far("w1", w1_dst, k)
        w_ready("w1", w1_dst, k)
        hidden(k)
        w_from_pair("w2", w2_dst, k - 1)
        w2_inner(k)
        relay(k - 1)
    x_ready(1)
    x_load(1)
    norm()
    hidden(4)
    w_from_pair("w2", w2_dst, 3)
    w_from_inner("w2", w2_dst, 0)
    w_from_far("w2", w2_dst, 0)
    relay(3)
    hidden(5)
    w_from_inner("w2", w2_dst, 1)
    w_from_far("w2", w2_dst, 1)
    relay(4)
    for k in range(CHUNKS):
        h_ready(k)
        far_ready(k)
    partial_out(0)
    hidden(6)
    partial_out(1)
    w_from_inner("w2", w2_dst, 2)
    w_from_far("w2", w2_dst, 2)
    relay(5)
    hidden(7)
    partial_out(2)
    local_copy("xres", x_ref, zb.at[0])
    relay(6)
    w_from_inner("w2", w2_dst, 3)
    w_from_far("w2", w2_dst, 3)
    partial_out(3)
    for k in (4, 5):
        h_ready(k)
        far_ready(k)
    for n in range(CHUNKS):
        project(1, y1, n, range(ny), 0, 2, True)
    relay(7)
    h_ready(6)
    far_ready(6)
    for n in range(CHUNKS):
        project(1, y1, n, range(ny), 2, 3, False)
    h_ready(7)
    for n in range(CHUNKS):
        project(1, y1, n, (y, up, dn), 3, 4, False)
    local["xres"].wait()
    for n in range(CHUNKS):
        comm.arrive(("y", n), yr.at[n])
    far_ready(7)
    for n in range(CHUNKS):
        project(1, y1, n, (far,), 3, 4, False)
        cols = slice(n * NC, (n + 1) * NC)
        zb[1, :, cols] = (zb[0, :, cols].astype(jnp.float32) + (y1[n] + yr[n])).astype(jnp.bfloat16)
    local_copy("out", zb.at[1], out_ref)
    local["out"].wait()
    comm.finish()
    assert len(comm.ids) <= N_SEMS and len(local) <= 32


def solution(mesh):
    nx, ny = mesh.shape["row"] // 2, mesh.shape["col"]
    act_spec = P(None, ("dp", "row"), "col")

    def per_device(x_blk, gamma_blk, w_in_blk, w_out_blk):
        mbs, toks, D = x_blk.shape
        T = mbs * toks
        KR, FL = w_in_blk.shape
        R2, N = w_out_blk.shape
        bf16, f32 = jnp.bfloat16, jnp.float32
        any_spec = pl.BlockSpec(memory_space=pl.ANY)
        vmem_spec = pl.BlockSpec(memory_space=pltpu.VMEM)
        NC = N // CHUNKS
        flops = 2 * 2 * T * (ny * D) * (FL // 2) * 2
        out, _ = pl.pallas_call(
            functools.partial(kernel, nx, ny),
            out_shape=(jax.ShapeDtypeStruct((T, N), bf16), jax.ShapeDtypeStruct((2, ny, T, D), bf16)),
            in_specs=[any_spec, vmem_spec, any_spec, any_spec],
            out_specs=(any_spec, any_spec),
            scratch_shapes=[
                pltpu.VMEM((ny, T, D), bf16),
                pltpu.VMEM((CHUNKS, 2 * nx * KR, FL // 2 // CHUNKS), bf16),
                pltpu.VMEM((CHUNKS, nx * R2, NC), bf16),
                pltpu.VMEM((2, ny, T, FL // 2), bf16),
                pltpu.VMEM((CHUNKS, T, NC), f32),
                pltpu.VMEM((CHUNKS, T, NC), f32),
                pltpu.VMEM((CHUNKS, T, NC), f32),
                pltpu.VMEM((ny, 1, D), f32),
                pltpu.SemaphoreType.DMA((N_SEMS,)),
                pltpu.SemaphoreType.DMA((N_SEMS,)),
                pltpu.SemaphoreType.DMA((32,)),
            ],
            compiler_params=pltpu.CompilerParams(collective_id=0, has_side_effects=True, vmem_limit_bytes=67043328),
            cost_estimate=pl.CostEstimate(flops=flops, bytes_accessed=64 * T * D, transcendentals=T * FL),
            name="ln_mlp",
        )(x_blk.reshape(T, D), gamma_blk.reshape(1, D), w_in_blk, w_out_blk)
        return out.reshape(x_blk.shape)

    return jax.shard_map(per_device, mesh=mesh, in_specs=(act_spec, P("col"), P("row", "col"), P("row", "col")), out_specs=act_spec, check_vma=False)
```

time: 569 us -> 224 us (0.39)
  waiting for transfers between devices: 489 us -> 0 us
  Pallas kernels: 0 us -> 221 us
  matrix products: 50.7 us -> 0 us
  between operations: 13.2 us -> 0.01 us
  blocking collectives: 11.2 us -> 0 us
    all_gather x4 -> x0, waiting for transfers between devices: 488 us -> none  [the longest x1 157 us: per_device(): w_in_panel = lax.all_gather(w_in_blk, 'row', axis=0, tiled=True)]
    pallas_call x0 -> x1, Pallas kernels: none -> 221 us  [per_device(): pl.pallas_call(functools.partial(kernel, nx, ny), out_shape=(jax.ShapeDty...]
    dot_general x2 -> x0, matrix products: 50.7 us -> none  [the longest x1 25.4 us: per_device(): branch = jnp.dot(h_panel, w_out_panel, preferred_element_type=jnp.float32)]
    psum x1 -> x0, blocking collectives: 11.2 us -> none  [per_device(): row_stats = lax.psum(row_stats, 'col')]
  transfers between devices with their start and end apart: 4 -> 0, of which waited for: 4 -> 0; matrix products, arithmetic and copies ran while one was open for 4% -> 0% of each run, Pallas kernels for 0% -> 0%
where the time goes in v1:
time: 224 us
  Pallas kernels  221 us (99%)
  local copies, waits for them, and re-layouts  2.26 us (1%)
    pallas_call x1, Pallas kernels, per_device(): pl.pallas_call(functools.partial(kernel, nx, ny), out_shape=(jax.ShapeDty...  221 us

profile of v1, /device:TPU:97, one launch (start us, length us, event | category | flops | bytes accessed | tf_op | source)
XLA Modules:
  0.0 223.5 jit_solution(11127885232556843482)
XLA Ops:
  0.0 221.3 %ln_mlp.1 = (bf16[512,1024]{1,0:T(8,128)(2,1)}, bf16[2,4,512,1024]{3,2,1,0:T(8,128)(2,1)}) custom-call(bf16[512,1024]{1,0:T(8,128)(2,1)} %bitcast.4, f32[1,1024]{1,0:T(1,128)} %bitcast.5, bf16[512,4096]{1,0:T(8,128)(2,1)} %w1_ref.1, bf16[2048,1024]{1,0:T(8,128)(2,1)} %w2_ref.1), custom_call_target="tpu_custom_call" | custom-call | flops 34359738368 | bytes 33554432 | tf_op jit(solution)/shard_map/ln_mlp/pallas_call | solution.py:333
  221.3 2.3 %copy.6 = bf16[2,256,1024]{2,1,0:T(8,128)(2,1)} copy(bf16[2,256,1024]{2,1,0:T(8,128)(2,1)} %bitcast.3) | data formatting | bytes 2097152

commit v2 on v1

v2 whole, which is shorter than its diff:
```python
import functools

import jax
import jax.numpy as jnp
from jax import lax
from jax.experimental import pallas as pl
from jax.experimental.pallas import tpu as pltpu
from jax.sharding import PartitionSpec as P

LN_EPS = 1e-5
MESH = pl.DeviceIdType.MESH
CHUNKS = 4
N_SEMS = 160
GELU_C = 0.7978845608028654


class Comm:
    def __init__(self, send_sems, recv_sems, some_peer):
        self.send_sems, self.recv_sems, self.some_peer = send_sems, recv_sems, some_peer
        self.ids, self.sent = {}, []

    def _id(self, key):
        return self.ids.setdefault(key, len(self.ids))

    def send(self, key, src, dst, dev):
        i = self._id(key)
        copy = pltpu.make_async_remote_copy(
            src_ref=src, dst_ref=dst, send_sem=self.send_sems.at[i], recv_sem=self.recv_sems.at[i], device_id=dev, device_id_type=MESH
        )
        copy.start()
        self.sent.append(copy)

    def arrive(self, key, ref):
        i = self._id(key)
        pltpu.make_async_remote_copy(
            src_ref=ref, dst_ref=ref, send_sem=self.send_sems.at[i], recv_sem=self.recv_sems.at[i], device_id=self.some_peer, device_id_type=MESH
        ).wait_recv()

    def finish(self):
        for copy in self.sent:
            copy.wait_send()


def kernel(nx, ny, x_ref, gamma_ref, w1_ref, w2_ref, own_ref, got_ref, xland, zb, w1b, w2b, hb, y0, y1, gb, send_sems, recv_sems, loc_sems):
    T, D = x_ref.shape
    KR, FL = w1_ref.shape
    R2, N = w2_ref.shape
    FH = FL // 2
    FC = FH // CHUNKS
    NC = N // CHUNKS
    T2 = T // 2
    RH = R2 // 2
    T4 = T // 4
    pieces = [(n, 0, NC) for n in range(CHUNKS - 1)] + [(CHUNKS - 1, 0, NC // 2), (CHUNKS - 1, NC // 2, NC // 2)]
    seq = [(1, 0), (0, 0), (0, 1), (0, 2), (0, 3), (1, 1), (1, 2), (1, 3)]

    row, y = lax.axis_index("row"), lax.axis_index("col")
    x, c = row // 2, row % 2
    xp, xi = nx - 1 - x, x + 1 - 2 * (x % 2)
    xf = nx - 1 - xi
    g = x // (nx // 2)
    up, dn, far = (y + 1) % ny, (y + ny - 1) % ny, (y + 2) % ny
    PX, PI, PC = {"row": 2 * xp + c}, {"row": 2 * xi + c}, {"row": 2 * x + 1 - c}
    YP, YM, YF = {"col": up}, {"col": dn}, {"col": far}

    barrier = pltpu.get_barrier_semaphore()
    for peer in (PX, PI, PC, YP, YM, YF):
        pl.semaphore_signal(barrier, inc=1, device_id=peer, device_id_type=MESH)
    pl.semaphore_wait(barrier, 6)

    comm = Comm(send_sems, recv_sems, PC)
    local = {}

    def local_copy(key, src, dst):
        copy = pltpu.make_async_copy(src, dst, loc_sems.at[len(local)])
        copy.start()
        local[key] = copy

    def tok(half):
        return pl.ds(half * T2, T2)

    def w1_src(grp, j):
        q, s = j // 2, j % 2
        col = pl.multiple_of(q * R2 + grp * RH + s * FC, FC)
        return w1_ref.at[:, pl.ds(col, FC)]

    def w1_dst(j, xx, cc):
        return w1b.at[j, pl.ds(pl.multiple_of((2 * xx + cc) * KR, KR), KR), :]

    def w2_src(grp, p):
        n, lo, size = pieces[p]
        return w2_ref.at[pl.ds(pl.multiple_of(grp * RH, RH), RH), pl.ds(n * NC + lo, size)]

    def w2_dst(p, xx, cc):
        n, lo, size = pieces[p]
        return w2b.at[n, pl.ds(pl.multiple_of((2 * xx + cc) * RH, RH), RH), pl.ds(lo, size)]

    def xl(h, yy, half):
        return xland.at[h, yy, tok(half), :]

    def xq(h, yy, quarter):
        return xland.at[h, yy, pl.ds(quarter * T4, T4), :]

    def hs(k, yy, half):
        h, j = seq[k]
        return hb.at[h, yy, tok(half), pl.ds(j * FC, FC)]

    for quarter in (2, 0, 3, 1):
        comm.send(("xp", quarter), x_ref.at[pl.ds(quarter * T4, T4), :], xq(0, y, quarter), PX)
    for a, b in ((0, 1), (1, 0)):
        comm.send(("x1P", a), x_ref.at[tok(a), :], xl(1, y, a), YP)
        comm.send(("x1M", b), x_ref.at[tok(b), :], xl(1, y, b), YM)

    def w1_outer(j):
        comm.send(("w1x", j), w1_src(1 - g, j), w1_dst(j, x, c), PX)

    def w1_inner(j):
        comm.send(("w1i", j), w1_src(g, j), w1_dst(j, x, c), PI)

    def w2_inner(p):
        comm.send(("w2i", p), w2_src(g, p), w2_dst(p, x, c), PI)

    w1_outer(0)
    for j in (0, 1, 2):
        w1_inner(j)
    for j in range(CHUNKS):
        comm.send(("w1c", 0, j), w1_src(g, j), w1_dst(j, x, c), PC)
        local_copy(("w1", j), w1_src(g, j), w1_dst(j, x, c))
    for yk, dev in (("P", YP), ("M", YM), ("F", YF)):
        comm.send(("g" + yk,), gamma_ref, gb.at[y], dev)
    local_copy("g", gamma_ref, gb.at[y])
    for p in range(len(pieces)):
        comm.send(("w2c", 0, p), w2_src(g, p), w2_dst(p, x, c), PC)
        local_copy(("w2", p), w2_src(g, p), w2_dst(p, x, c))

    def w_from_inner(w, dst, j):
        comm.arrive((w + "i", j), dst(j, xi, c))
        comm.send((w + "c", 1, j), dst(j, xi, c), dst(j, xi, c), PC)

    def w_from_pair(w, dst, j):
        comm.arrive((w + "x", j), dst(j, xp, c))
        comm.send((w + "f", j), dst(j, xp, c), dst(j, xp, c), PI)
        comm.send((w + "c", 2, j), dst(j, xp, c), dst(j, xp, c), PC)

    def w_from_far(w, dst, j):
        comm.arrive((w + "f", j), dst(j, xf, c))
        comm.send((w + "c", 3, j), dst(j, xf, c), dst(j, xf, c), PC)

    def w_ready(w, dst, j):
        for i, xx in enumerate((x, xi, xp, xf)):
            comm.arrive((w + "c", i, j), dst(j, xx, 1 - c))
        local[(w, j)].wait()

    def x_load(h):
        local_copy(("z", h, 0), xland.at[0, y] if h == 0 else x_ref, zb.at[h, y])
        for i, yy in enumerate((up, dn, far)):
            local_copy(("z", h, i + 1), xland.at[h, yy], zb.at[h, yy])
        for i in range(4):
            local[("z", h, i)].wait()

    def norm(h):
        rb = 32

        def body(i, carry):
            rows = pl.ds(pl.multiple_of(i * rb, rb), rb)
            s = jnp.zeros((rb, 1), jnp.float32)
            q = jnp.zeros((rb, 1), jnp.float32)
            for yy in range(ny):
                v = zb[h, yy, rows, :].astype(jnp.float32)
                s += jnp.sum(v, axis=-1, keepdims=True)
                q += jnp.sum(v * v, axis=-1, keepdims=True)
            mu = s / (ny * D)
            var = q / (ny * D) - mu * mu
            inv = lax.rsqrt(var + LN_EPS)
            for yy in range(ny):
                v = zb[h, yy, rows, :].astype(jnp.float32)
                zb[h, yy, rows, :] = ((v - mu) * inv * gb[yy]).astype(jnp.bfloat16)
            return carry

        lax.fori_loop(0, T // rb, body, 0)

    def hidden(k):
        h, j = seq[k]
        mb = T2

        def body(i, carry):
            rows = pl.ds(pl.multiple_of(i * mb, mb), mb)
            u = jnp.zeros((mb, FC), jnp.float32)
            for yy in range(ny):
                u += jnp.dot(zb[h, yy, rows, :], w1b[j, yy * D : (yy + 1) * D, :], preferred_element_type=jnp.float32)
            cdf = 0.5 * (1.0 + jnp.tanh(GELU_C * (u + 0.044715 * (u * u * u))))
            hb[h, y, rows, j * FC : (j + 1) * FC] = (u * cdf).astype(jnp.bfloat16)
            return carry

        lax.fori_loop(0, T // mb, body, 0)
        for a, b in ((0, 1), (1, 0)):
            comm.send(("hP", k, a), hs(k, y, a), hs(k, y, a), YP)
            comm.send(("hM", k, b), hs(k, y, b), hs(k, y, b), YM)

    def relay(k):
        comm.arrive(("hP", k, 0), hs(k, dn, 0))
        comm.send(("fP", k), hs(k, dn, 0), hs(k, dn, 0), YP)
        comm.arrive(("hM", k, 1), hs(k, up, 1))
        comm.send(("fM", k), hs(k, up, 1), hs(k, up, 1), YM)

    def h_ready(k):
        comm.arrive(("hP", k, 1), hs(k, dn, 1))
        comm.arrive(("hM", k, 0), hs(k, up, 0))

    def far_ready(k):
        comm.arrive(("fP", k), hs(k, far, 0))
        comm.arrive(("fM", k), hs(k, far, 1))

    def project(h, acc, p, yys, j0, j1, first, rows=slice(None)):
        n, c0, size = pieces[p]
        cols = slice(c0, c0 + size)
        for yy in yys:
            lo, depth = j0 * FC, (j1 - j0) * FC
            base = yy * FH + lo
            if not isinstance(base, int):
                base = pl.multiple_of(base, FC)
            d = jnp.dot(hb[h, yy, rows, lo : lo + depth], w2b[n, pl.ds(base, depth), cols], preferred_element_type=jnp.float32)
            if first:
                acc[n, rows, cols] = d
                first = False
            else:
                acc[n, rows, cols] += d

    def got_at(p):
        n, c0, size = pieces[p]
        return got_ref.at[:, pl.ds(n * NC + c0, size)]

    def partial_out(p):
        n, c0, size = pieces[p]
        w_ready("w2", w2_dst, p)
        project(0, y0, p, range(ny), 0, CHUNKS, True)
        comm.send(("y", p), y0.at[n, :, pl.ds(c0, size)], got_at(p), PX)

    comm.arrive(("x1P", 0), xl(1, dn, 0))
    comm.send(("eP",), xl(1, dn, 0), xl(0, dn, 0), PX)
    comm.arrive(("x1M", 1), xl(1, up, 1))
    comm.send(("eM",), xl(1, up, 1), xl(0, up, 1), PX)
    for j in (1, 2, 3):
        w1_outer(j)
    for p in range(len(pieces)):
        comm.send(("w2x", p), w2_src(1 - g, p), w2_dst(p, x, c), PX)
    for quarter, dev in ((2, YP), (0, YM), (3, YP), (1, YM)):
        comm.arrive(("xp", quarter), xq(0, y, quarter))
        comm.send(("x0", quarter), xq(0, y, quarter), xq(0, y, quarter), dev)
    comm.send(("x1p",), xl(1, dn, 0), xl(1, dn, 0), YP)
    comm.send(("x1m",), xl(1, up, 1), xl(1, up, 1), YM)
    w_from_inner("w1", w1_dst, 0)
    w_from_inner("w1", w1_dst, 1)
    w_from_pair("w1", w1_dst, 0)
    w1_inner(3)
    w2_inner(0)
    for quarter in (2, 3):
        comm.arrive(("x0", quarter), xq(0, dn, quarter))
    comm.send(("x0p",), xl(0, dn, 1), xl(0, dn, 1), YP)
    for quarter in (0, 1):
        comm.arrive(("x0", quarter), xq(0, up, quarter))
    comm.send(("x0m",), xl(0, up, 0), xl(0, up, 0), YM)
    w_from_inner("w1", w1_dst, 2)

    local["g"].wait()
    for yk, yy in (("P", dn), ("M", up), ("F", far)):
        comm.arrive(("g" + yk,), gb.at[yy])
    comm.arrive(("x1P", 1), xl(1, dn, 1))
    comm.arrive(("x1M", 0), xl(1, up, 0))
    comm.arrive(("x1p",), xl(1, far, 0))
    comm.arrive(("x1m",), xl(1, far, 1))
    x_load(1)
    norm(1)
    w_from_far("w1", w1_dst, 0)
    w_ready("w1", w1_dst, 0)
    hidden(0)
    comm.arrive(("eP",), xl(0, dn, 0))
    comm.arrive(("eM",), xl(0, up, 1))
    comm.arrive(("x0p",), xl(0, far, 1))
    comm.arrive(("x0m",), xl(0, far, 0))
    x_load(0)
    norm(0)
    hidden(1)
    w_from_inner("w1", w1_dst, 3)
    w_from_pair("w1", w1_dst, 1)
    relay(0)
    w_from_pair("w1", w1_dst, 2)
    w_from_far("w1", w1_dst, 1)
    w_ready("w1", w1_dst, 1)
    hidden(2)
    relay(1)
    w_from_pair("w1", w1_dst, 3)
    w2_inner(1)
    w_from_far("w1", w1_dst, 2)
    w_ready("w1", w1_dst, 2)
    hidden(3)
    w_from_pair("w2", w2_dst, 0)
    relay(2)
    w_from_far("w1", w1_dst, 3)
    w_ready("w1", w1_dst, 3)
    hidden(4)
    w_from_pair("w2", w2_dst, 1)
    w2_inner(2)
    relay(3)
    hidden(5)
    w_from_pair("w2", w2_dst, 2)
    w2_inner(3)
    w_from_inner("w2", w2_dst, 0)
    w_from_far("w2", w2_dst, 0)
    w_from_pair("w2", w2_dst, 3)
    w2_inner(4)
    w_from_pair("w2", w2_dst, 4)
    relay(4)
    hidden(6)
    w_from_inner("w2", w2_dst, 1)
    w_from_far("w2", w2_dst, 1)
    for k in range(5):
        h_ready(k)
        far_ready(k)
    partial_out(0)
    partial_out(1)
    relay(5)
    hidden(7)
    w_from_inner("w2", w2_dst, 2)
    w_from_far("w2", w2_dst, 2)
    partial_out(2)
    relay(6)
    h_ready(5)
    far_ready(5)
    w_from_inner("w2", w2_dst, 3)
    w_from_far("w2", w2_dst, 3)
    partial_out(3)
    for p in (0, 1, 2):
        project(1, y1, p, range(ny), 0, 2, True)
    w_from_inner("w2", w2_dst, 4)
    w_from_far("w2", w2_dst, 4)
    partial_out(4)
    relay(7)
    for p in (3, 4):
        project(1, y1, p, range(ny), 0, 2, True)
    h_ready(6)
    far_ready(6)
    for p in range(len(pieces)):
        project(1, y1, p, range(ny), 2, 3, False)
    h_ready(7)
    for p in range(len(pieces)):
        project(1, y1, p, (y, up, dn), 3, 4, False)
    far_ready(7)
    for n in range(CHUNKS):
        for p, piece in enumerate(pieces):
            if piece[0] == n:
                project(1, y1, p, (far,), 3, 4, False)
        local_copy(("out", n), y1.at[n], own_ref.at[:, pl.ds(n * NC, NC)])
    for p in range(len(pieces)):
        comm.arrive(("y", p), got_at(p))
    for n in range(CHUNKS):
        local[("out", n)].wait()
    comm.finish()
    assert len(comm.ids) <= N_SEMS and len(local) <= 32


def solution(mesh):
    nx, ny = mesh.shape["row"] // 2, mesh.shape["col"]
    act_spec = P(None, ("dp", "row"), "col")

    def per_device(x_blk, gamma_blk, w_in_blk, w_out_blk):
        mbs, toks, D = x_blk.shape
        T = mbs * toks
        KR, FL = w_in_blk.shape
        R2, N = w_out_blk.shape
        bf16, f32 = jnp.bfloat16, jnp.float32
        any_spec = pl.BlockSpec(memory_space=pl.ANY)
        vmem_spec = pl.BlockSpec(memory_space=pltpu.VMEM)
        NC = N // CHUNKS
        flops = 2 * 2 * T * (ny * D) * (FL // 2) * 2
        own, got, _ = pl.pallas_call(
            functools.partial(kernel, nx, ny),
            out_shape=(jax.ShapeDtypeStruct((T, N), f32), jax.ShapeDtypeStruct((T, N), f32), jax.ShapeDtypeStruct((2, ny, T, D), bf16)),
            in_specs=[any_spec, vmem_spec, any_spec, any_spec],
            out_specs=(any_spec, any_spec, any_spec),
            scratch_shapes=[
                pltpu.VMEM((2, ny, T, D), bf16),
                pltpu.VMEM((CHUNKS, 2 * nx * KR, FL // 2 // CHUNKS), bf16),
                pltpu.VMEM((CHUNKS, nx * R2, NC), bf16),
                pltpu.VMEM((2, ny, T, FL // 2), bf16),
                pltpu.VMEM((CHUNKS, T, NC), f32),
                pltpu.VMEM((CHUNKS, T, NC), f32),
                pltpu.VMEM((ny, 1, D), f32),
                pltpu.SemaphoreType.DMA((N_SEMS,)),
                pltpu.SemaphoreType.DMA((N_SEMS,)),
                pltpu.SemaphoreType.DMA((32,)),
            ],
            compiler_params=pltpu.CompilerParams(collective_id=0, has_side_effects=True, vmem_limit_bytes=67043328),
            cost_estimate=pl.CostEstimate(flops=flops, bytes_accessed=64 * T * D, transcendentals=T * FL),
            name="ln_mlp",
        )(x_blk.reshape(T, D), gamma_blk.reshape(1, D), w_in_blk, w_out_blk)
        out = x_blk.reshape(T, D).astype(f32) + (own + got)
        return out.astype(bf16).reshape(x_blk.shape)

    return jax.shard_map(per_device, mesh=mesh, in_specs=(act_spec, P("col"), P("row", "col"), P("row", "col")), out_specs=act_spec, check_vma=False)
```

time: 224 us -> 221 us (0.987)
  other arithmetic: 0 us -> 4.07 us
  Pallas kernels: 221 us -> 217 us
  local copies, waits for them, and re-layouts: 2.26 us -> 0 us
    pallas_call x1, Pallas kernels: 221 us -> 217 us  [per_device(): pl.pallas_call(functools.partial(kernel, nx, ny), out_shape=(jax.ShapeDty...]
    convert_element_type x0 -> x1, other arithmetic: none -> 4.07 us  [per_device(): return out.astype(bf16).reshape(x_blk.shape)]
    unnamed x1 -> x0, local copies, waits for them, and re-layouts: 2.26 us -> none
where the time goes in v2:
time: 221 us
  Pallas kernels  217 us (98%)
  other arithmetic  4.07 us (2%)
    pallas_call x1, Pallas kernels, per_device(): pl.pallas_call(functools.partial(kernel, nx, ny), out_shape=(jax.ShapeDty...  217 us

profile of v2, /device:TPU:97, one launch (start us, length us, event | category | flops | bytes accessed | tf_op | source)
XLA Modules:
  0.0 221.1 jit_solution(4053513187447929509)
XLA Ops:
  0.0 217.1 %ln_mlp.1 = (f32[512,1024]{1,0:T(8,128)}, f32[512,1024]{1,0:T(8,128)}, bf16[2,4,512,1024]{3,2,1,0:T(8,128)(2,1)}) custom-call(bf16[512,1024]{1,0:T(8,128)(2,1)} %bitcast.4, f32[1,1024]{1,0:T(1,128)} %bitcast.5, bf16[512,4096]{1,0:T(8,128)(2,1)} %w1_ref.1, bf16[2048,1024]{1,0:T(8,128)(2,1)} %w2_ref.1), custom_call_target="tpu_custom_call" | custom-call | flops 34359738368 | bytes 33554432 | tf_op jit(solution)/shard_map/ln_mlp/pallas_call | solution.py:376
  217.1 4.1 %add_convert_fusion = bf16[512,1024]{1,0:T(8,128)(2,1)} fusion(f32[512,1024]{1,0:T(8,128)} %get-tuple-element.7, f32[512,1024]{1,0:T(8,128)} %get-tuple-element.8, bf16[2,256,1024]{2,1,0:T(8,128)(2,1)} %param.4), kind=kLoop, calls=%fused_computation | loop fusion | flops 2097152 | bytes 6291456 | tf_op jit(solution)/shard_map/convert_element_type | solution.py:398

commit v3 on v1

--- a/solution.py
+++ b/solution.py
@@ -10,7 +10,7 @@
 LN_EPS = 1e-5
 MESH = pl.DeviceIdType.MESH
 CHUNKS = 4
-N_SEMS = 144
+N_SEMS = 176
 GELU_C = 0.7978845608028654
 
 
@@ -50,6 +50,11 @@
     NC = N // CHUNKS
     T2 = T // 2
     RH = R2 // 2
+    T4 = T // 4
+    pieces = [(n, 0, NC) for n in range(CHUNKS - 1)] + [(CHUNKS - 1, 0, NC // 2), (CHUNKS - 1, NC // 2, NC // 2)]
+    wpieces = [(j, 0, FC) for j in range(CHUNKS - 1)] + [(CHUNKS - 1, 0, FC // 2), (CHUNKS - 1, FC // 2, FC // 2)]
+    NP = len(pieces)
+    seq = [(h, j) for h in (0, 1) for j in range(CHUNKS)]
 
     row, y = lax.axis_index("row"), lax.axis_index("col")
     x, c = row // 2, row % 2
@@ -76,44 +81,48 @@
     def tok(half):
         return pl.ds(half * T2, T2)
 
-    def w1_src(grp, j):
+    def w1_src(grp, p):
+        j, lo, size = wpieces[p]
         q, s = j // 2, j % 2
-        col = pl.multiple_of(q * R2 + grp * RH + s * FC, FC)
-        return w1_ref.at[:, pl.ds(col, FC)]
-
-    def w1_dst(j, xx, cc):
-        return w1b.at[j, pl.ds(pl.multiple_of((2 * xx + cc) * KR, KR), KR), :]
-
-    def w2_src(grp, n):
-        return w2_ref.at[pl.ds(pl.multiple_of(grp * RH, RH), RH), pl.ds(n * NC, NC)]
-
-    def w2_dst(n, xx, cc):
-        return w2b.at[n, pl.ds(pl.multiple_of((2 * xx + cc) * RH, RH), RH), :]
+        col = pl.multiple_of(q * R2 + grp * RH + s * FC + lo, size)
+        return w1_ref.at[:, pl.ds(col, size)]
+
+    def w1_dst(p, xx, cc):
+        j, lo, size = wpieces[p]
+        return w1b.at[j, pl.ds(pl.multiple_of((2 * xx + cc) * KR, KR), KR), pl.ds(lo, size)]
+
+    def w2_src(grp, p):
+        n, lo, size = pieces[p]
+        return w2_ref.at[pl.ds(pl.multiple_of(grp * RH, RH), RH), pl.ds(n * NC + lo, size)]
+
+    def w2_dst(p, xx, cc):
+        n, lo, size = pieces[p]
+        return w2b.at[n, pl.ds(pl.multiple_of((2 * xx + cc) * RH, RH), RH), pl.ds(lo, size)]
 
     def xl(h, yy, half):
         return xland.at[h, yy, tok(half), :]
 
+    def xq(h, yy, quarter):
+        return xland.at[h, yy, pl.ds(quarter * T4, T4), :]
+
     def hs(k, yy, half):
-        h, j = divmod(k, CHUNKS)
+        h, j = seq[k]
         return hb.at[h, yy, tok(half), pl.ds(j * FC, FC)]
 
-    for half in (0, 1):
-        comm.send(("xp", half), x_ref.at[tok(half), :], xl(0, y, half), PX)
-    for a, b in ((0, 1), (1, 0)):
-        comm.send(("x1P", a), x_ref.at[tok(a), :], xl(1, y, a), YP)
-        comm.send(("x1M", b), x_ref.at[tok(b), :], xl(1, y, b), YM)
-    for j in range(CHUNKS):
-        comm.send(("w1x", j), w1_src(1 - g, j), w1_dst(j, x, c), PX)
-        comm.send(("w1i", j), w1_src(g, j), w1_dst(j, x, c), PI)
-        comm.send(("w1c", 0, j), w1_src(g, j), w1_dst(j, x, c), PC)
-        local_copy(("w1", j), w1_src(g, j), w1_dst(j, x, c))
-    for yk, dev in (("P", YP), ("M", YM), ("F", YF)):
-        comm.send(("g" + yk,), gamma_ref, gb.at[y], dev)
-    local_copy("g", gamma_ref, gb.at[y])
-    for n in range(CHUNKS):
-        comm.send(("w2x", n), w2_src(1 - g, n), w2_dst(n, x, c), PX)
-        comm.send(("w2c", 0, n), w2_src(g, n), w2_dst(n, x, c), PC)
-        local_copy(("w2", n), w2_src(g, n), w2_dst(n, x, c))
+    def w1_inner(p):
+        comm.send(("w1i", p), w1_src(g, p), w1_dst(p, x, c), PI)
+
+    def w2_inner(p):
+        comm.send(("w2i", p), w2_src(g, p), w2_dst(p, x, c), PI)
+
+    for quarter in (0, 2, 1, 3):
+        comm.send(("xp", quarter), x_ref.at[pl.ds(quarter * T4, T4), :], xq(0, y, quarter), PX)
+    comm.send(("x1P",), x_ref.at[tok(1), :], xl(1, y, 1), YP)
+    comm.send(("x1M",), x_ref.at[tok(0), :], xl(1, y, 0), YM)
+    for p in (0, 1, 2, 3):
+        w1_inner(p)
+    for p in range(NP):
+        comm.send(("w1x", p), w1_src(1 - g, p), w1_dst(p, x, c), PX)
 
     def w_from_inner(w, dst, j):
         comm.arrive((w + "i", j), dst(j, xi, c))
@@ -134,10 +143,7 @@
         local[(w, j)].wait()
 
     def x_load(h):
-        if h == 0:
-            local_copy(("z", h, 0), xland.at[0, y], zb.at[y])
-        else:
-            local_copy(("z", h, 0), x_ref, zb.at[y])
+        local_copy(("z", h, 0), xland.at[0, y] if h == 0 else x_ref, zb.at[y])
         for i, yy in enumerate((up, dn, far)):
             local_copy(("z", h, i + 1), xland.at[h, yy], zb.at[yy])
         for i in range(4):
@@ -165,7 +171,7 @@
         lax.fori_loop(0, T // rb, body, 0)
 
     def hidden(k):
-        h, j = divmod(k, CHUNKS)
+        h, j = seq[k]
         mb = T2
 
         def body(i, carry):
@@ -196,105 +202,162 @@
         comm.arrive(("fP", k), hs(k, far, 0))
         comm.arrive(("fM", k), hs(k, far, 1))
 
-    def project(h, acc, n, yys, j0, j1, first):
+    def project(h, acc, n, yys, j0, j1, first, cols=slice(None)):
         for yy in yys:
-            lo, size = j0 * FC, (j1 - j0) * FC
+            lo, depth = j0 * FC, (j1 - j0) * FC
             base = yy * FH + lo
             if not isinstance(base, int):
                 base = pl.multiple_of(base, FC)
-            d = jnp.dot(hb[h, yy, :, lo : lo + size], w2b[n, pl.ds(base, size), :], preferred_element_type=jnp.float32)
+            d = jnp.dot(hb[h, yy, :, lo : lo + depth], w2b[n, pl.ds(base, depth), cols], preferred_element_type=jnp.float32)
             if first:
-                acc[n] = d
+                acc[n, :, cols] = d
                 first = False
             else:
-                acc[n] += d
-
-    def partial_out(n):
-        w_ready("w2", w2_dst, n)
-        project(0, y0, n, range(ny), 0, CHUNKS, True)
-        comm.send(("y", n), y0.at[n], yr.at[n], PX)
-
-    comm.arrive(("xp", 0), xl(0, y, 0))
-    comm.send(("x0P", 0), xl(0, y, 0), xl(0, y, 0), YP)
-    comm.arrive(("xp", 1), xl(0, y, 1))
-    comm.send(("x0P", 1), xl(0, y, 1), xl(0, y, 1), YP)
-    comm.send(("x0M", 1), xl(0, y, 1), xl(0, y, 1), YM)
-    comm.send(("x0M", 0), xl(0, y, 0), xl(0, y, 0), YM)
+                acc[n, :, cols] += d
+
+    def partial_out(p):
+        n, c0, size = pieces[p]
+        cols = slice(c0, c0 + size)
+        for i, xx in enumerate((x, xi, xp)):
+            comm.arrive(("w2c", i, p), w2_dst(p, xx, 1 - c))
+        local[("w2", p)].wait()
+        project(0, y0, n, (x, xi, xp), 0, CHUNKS, True, cols)
+        comm.arrive(("w2c", 3, p), w2_dst(p, xf, 1 - c))
+        project(0, y0, n, (xf,), 0, CHUNKS, False, cols)
+        comm.send(("y", p), y0.at[n, :, pl.ds(c0, size)], yr.at[n, :, pl.ds(c0, size)], PX)
+
+    def x_relay(quarter):
+        comm.arrive(("xp", quarter), xq(0, y, quarter))
+        comm.send(("x0P", quarter), xq(0, y, quarter), xq(0, y, quarter), YP)
+        comm.send(("x0M", quarter), xq(0, y, quarter), xq(0, y, quarter), YM)
+
+    def x_up(quarter):
+        comm.arrive(("x0P", quarter), xq(0, dn, quarter))
+        comm.send(("x0p", quarter), xq(0, dn, quarter), xq(0, dn, quarter), YP)
+
+    def x_down(quarter):
+        comm.arrive(("x0M", quarter), xq(0, up, quarter))
+        comm.send(("x0m", quarter), xq(0, up, quarter), xq(0, up, quarter), YM)
+
+    x_relay(0)
+    for yk, dev in (("P", YP), ("M", YM), ("F", YF)):
+        comm.send(("g" + yk,), gamma_ref, gb.at[y], dev)
+    local_copy("g", gamma_ref, gb.at[y])
+    x_relay(2)
+    for p in range(NP):
+        comm.send(("w1c", 0, p), w1_src(g, p), w1_dst(p, x, c), PC)
+        local_copy(("w1", p), w1_src(g, p), w1_dst(p, x, c))
+    x_up(0)
+    x_relay(1)
+    x_down(2)
+    x_relay(3)
     w_from_inner("w1", w1_dst, 0)
-    for h in (0, 1):
-        hk = "x%d" % h
-        comm.arrive((hk + "P", 0), xl(h, dn, 0))
-        comm.send((hk + "p",), xl(h, dn, 0), xl(h, dn, 0), YP)
-        comm.arrive((hk + "M", 1), xl(h, up, 1))
-        comm.send((hk + "m",), xl(h, up, 1), xl(h, up, 1), YM)
-        w_from_pair("w1", w1_dst, h)
-        w_from_inner("w1", w1_dst, h + 1)
+    w_from_inner("w1", w1_dst, 1)
+    x_up(1)
+    comm.send(("eP",), xl(0, dn, 0), xl(1, dn, 0), PX)
+    comm.arrive(("x1P",), xl(1, dn, 1))
+    comm.send(("x1p",), xl(1, dn, 1), xl(1, dn, 1), YP)
+    x_down(3)
+    comm.send(("eM",), xl(0, up, 1), xl(1, up, 1), PX)
+    comm.arrive(("x1M",), xl(1, up, 0))
+    comm.send(("x1m",), xl(1, up, 0), xl(1, up, 0), YM)
+    w_from_pair("w1", w1_dst, 0)
+    for p in range(NP):
+        comm.send(("w2x", p), w2_src(1 - g, p), w2_dst(p, x, c), PX)
+    w_from_inner("w1", w1_dst, 2)
+    w_from_pair("w1", w1_dst, 1)
+    w1_inner(4)
     w_from_inner("w1", w1_dst, 3)
-    w_from_pair("w1", w1_dst, 2)
-
-    def x_ready(h):
-        hk = "x%d" % h
-        comm.arrive((hk + "P", 1), xl(h, dn, 1))
-        comm.arrive((hk + "M", 0), xl(h, up, 0))
-        comm.arrive((hk + "p",), xl(h, far, 0))
-        comm.arrive((hk + "m",), xl(h, far, 1))
 
     local["g"].wait()
     for yk, yy in (("P", dn), ("M", up), ("F", far)):
         comm.arrive(("g" + yk,), gb.at[yy])
-    x_ready(0)
+    for quarter in (2, 3):
+        comm.arrive(("x0P", quarter), xq(0, dn, quarter))
+        comm.arrive(("x0m", quarter), xq(0, far, quarter))
+    for quarter in (0, 1):
+        comm.arrive(("x0M", quarter), xq(0, up, quarter))
+        comm.arrive(("x0p", quarter), xq(0, far, quarter))
     x_load(0)
     norm()
-
-    def w2_inner(n):
-        comm.send(("w2i", n), w2_src(g, n), w2_dst(n, x, c), PI)
-
     w_from_far("w1", w1_dst, 0)
     w_ready("w1", w1_dst, 0)
     hidden(0)
+    for p in range(NP):
+        comm.send(("w2c", 0, p), w2_src(g, p), w2_dst(p, x, c), PC)
+        local_copy(("w2", p), w2_src(g, p), w2_dst(p, x, c))
+    w_from_pair("w1", w1_dst, 2)
+    w_from_far("w1", w1_dst, 1)
+    w_ready("w1", w1_dst, 1)
+    hidden(1)
+    relay(0)
     w_from_pair("w1", w1_dst, 3)
+    w_from_inner("w1", w1_dst, 4)
+    w_from_pair("w1", w1_dst, 4)
     w2_inner(0)
-    for k in (1, 2, 3):
-        w_from_far("w1", w1_dst, k)
-        w_ready("w1", w1_dst, k)
-        hidden(k)
-        w_from_pair("w2", w2_dst, k - 1)
-        w2_inner(k)
-        relay(k - 1)
-    x_ready(1)
+    w2_inner(1)
+    w_from_far("w1", w1_dst, 2)
+    w_ready("w1", w1_dst, 2)
+    hidden(2)
+    relay(1)
+    w_from_far("w1", w1_dst, 3)
+    w_from_far("w1", w1_dst, 4)
+    w_ready("w1", w1_dst, 3)
+    w_ready("w1", w1_dst, 4)
+    hidden(3)
+    relay(2)
+    comm.arrive(("eP",), xl(1, dn, 0))
+    comm.arrive(("eM",), xl(1, up, 1))
+    comm.arrive(("x1p",), xl(1, far, 1))
+    comm.arrive(("x1m",), xl(1, far, 0))
     x_load(1)
     norm()
     hidden(4)
-    w_from_pair("w2", w2_dst, 3)
+    w_from_pair("w2", w2_dst, 0)
+    w_from_pair("w2", w2_dst, 1)
+    w2_inner(2)
+    relay(3)
+    hidden(5)
+    w_from_pair("w2", w2_dst, 2)
+    w2_inner(3)
     w_from_inner("w2", w2_dst, 0)
     w_from_far("w2", w2_dst, 0)
-    relay(3)
-    hidden(5)
+    w_from_pair("w2", w2_dst, 3)
+    w2_inner(4)
+    relay(4)
+    w_from_pair("w2", w2_dst, 4)
+    hidden(6)
     w_from_inner("w2", w2_dst, 1)
     w_from_far("w2", w2_dst, 1)
-    relay(4)
-    for k in range(CHUNKS):
+    for k in range(4):
         h_ready(k)
         far_ready(k)
     partial_out(0)
-    hidden(6)
     partial_out(1)
+    relay(5)
+    hidden(7)
+    local_copy("xres", x_ref, zb.at[0])
+    h_ready(4)
+    far_ready(4)
+    for n in (0, 1):
+        project(1, y1, n, range(ny), 0, 1, True)
     w_from_inner("w2", w2_dst, 2)
     w_from_far("w2", w2_dst, 2)
-    relay(5)
-    hidden(7)
     partial_out(2)
-    local_copy("xres", x_ref, zb.at[0])
     relay(6)
+    project(1, y1, 2, range(ny), 0, 1, True)
+    h_ready(5)
+    far_ready(5)
     w_from_inner("w2", w2_dst, 3)
     w_from_far("w2", w2_dst, 3)
     partial_out(3)
-    for k in (4, 5):
-        h_ready(k)
-        far_ready(k)
-    for n in range(CHUNKS):
-        project(1, y1, n, range(ny), 0, 2, True)
+    for n in (0, 1, 2):
+        project(1, y1, n, range(ny), 1, 2, False)
+    w_from_inner("w2", w2_dst, 4)
     relay(7)
+    w_from_far("w2", w2_dst, 4)
+    partial_out(4)
+    project(1, y1, 3, range(ny), 0, 2, True)
     h_ready(6)
     far_ready(6)
     for n in range(CHUNKS):
@@ -303,15 +366,17 @@
     for n in range(CHUNKS):
         project(1, y1, n, (y, up, dn), 3, 4, False)
     local["xres"].wait()
-    for n in range(CHUNKS):
-        comm.arrive(("y", n), yr.at[n])
+    for p in range(NP):
+        n, c0, size = pieces[p]
+        comm.arrive(("y", p), yr.at[n, :, pl.ds(c0, size)])
     far_ready(7)
     for n in range(CHUNKS):
         project(1, y1, n, (far,), 3, 4, False)
         cols = slice(n * NC, (n + 1) * NC)
         zb[1, :, cols] = (zb[0, :, cols].astype(jnp.float32) + (y1[n] + yr[n])).astype(jnp.bfloat16)
-    local_copy("out", zb.at[1], out_ref)
-    local["out"].wait()
+        local_copy(("out", n), zb.at[1, :, pl.ds(n * NC, NC)], out_ref.at[:, pl.ds(n * NC, NC)])
+    for n in range(CHUNKS):
+        local[("out", n)].wait()
     comm.finish()
     assert len(comm.ids) <= N_SEMS and len(local) <= 32
 

time: 224 us -> 213 us (0.951)
  Pallas kernels: 221 us -> 210 us
    pallas_call x1, Pallas kernels: 221 us -> 210 us  [per_device(): pl.pallas_call(functools.partial(kernel, nx, ny), out_shape=(jax.ShapeDty...]
where the time goes in v3:
time: 213 us; the launch traced here: 212 us
  Pallas kernels  210 us (99%)
  local copies, waits for them, and re-layouts  2.26 us (1%)
    pallas_call x1, Pallas kernels, per_device(): pl.pallas_call(functools.partial(kernel, nx, ny), out_shape=(jax.ShapeDty...  210 us

profile of v3, /device:TPU:97, one launch (start us, length us, event | category | flops | bytes accessed | tf_op | source)
XLA Modules:
  0.0 212.4 jit_solution(366241807203452978)
XLA Ops:
  0.0 210.2 %ln_mlp.1 = (bf16[512,1024]{1,0:T(8,128)(2,1)}, bf16[2,4,512,1024]{3,2,1,0:T(8,128)(2,1)}) custom-call(bf16[512,1024]{1,0:T(8,128)(2,1)} %bitcast.4, f32[1,1024]{1,0:T(1,128)} %bitcast.5, bf16[512,4096]{1,0:T(8,128)(2,1)} %w1_ref.1, bf16[2048,1024]{1,0:T(8,128)(2,1)} %w2_ref.1), custom_call_target="tpu_custom_call" | custom-call | flops 34359738368 | bytes 33554432 | tf_op jit(solution)/shard_map/ln_mlp/pallas_call | solution.py:398
  210.2 2.3 %copy.6 = bf16[2,256,1024]{2,1,0:T(8,128)(2,1)} copy(bf16[2,256,1024]{2,1,0:T(8,128)(2,1)} %bitcast.3) | data formatting | bytes 2097152

commit v4 on v3

--- a/solution.py
+++ b/solution.py
@@ -10,35 +10,51 @@
 LN_EPS = 1e-5
 MESH = pl.DeviceIdType.MESH
 CHUNKS = 4
-N_SEMS = 176
+N_RECV, N_SEND, N_LOCAL = 91, 6, 15
 GELU_C = 0.7978845608028654
+
+
+def arrival(key):
+    kind = key[0]
+    if kind in ("gP", "gM", "gF"):
+        return ("g",)
+    if kind in ("w1c", "w2c"):
+        return (kind, key[1] == 3 and kind == "w2c", key[2])
+    if (kind == "x0P" and key[1] >= 2) or (kind == "x0M" and key[1] < 2) or kind in ("x0p", "x0m"):
+        return ("x0",)
+    if kind in ("x1p", "x1m", "eP", "eM"):
+        return ("x1",)
+    if (kind == "hP" and key[2] == 1) or (kind == "hM" and key[2] == 0):
+        return ("h", key[1])
+    if kind in ("fP", "fM"):
+        return ("f", key[1])
+    if kind == "y":
+        return ("y",)
+    return key
 
 
 class Comm:
     def __init__(self, send_sems, recv_sems, some_peer):
         self.send_sems, self.recv_sems, self.some_peer = send_sems, recv_sems, some_peer
-        self.ids, self.sent = {}, []
-
-    def _id(self, key):
-        return self.ids.setdefault(key, len(self.ids))
+        self.recv_ids, self.send_ids = {}, {}
+
+    def _copy(self, group, arr, src, dst, dev):
+        i = self.send_ids.setdefault(group, len(self.send_ids))
+        j = self.recv_ids.setdefault(arr, len(self.recv_ids))
+        return pltpu.make_async_remote_copy(
+            src_ref=src, dst_ref=dst, send_sem=self.send_sems.at[i], recv_sem=self.recv_sems.at[j], device_id=dev, device_id_type=MESH
+        )
 
     def send(self, key, src, dst, dev):
-        i = self._id(key)
-        copy = pltpu.make_async_remote_copy(
-            src_ref=src, dst_ref=dst, send_sem=self.send_sems.at[i], recv_sem=self.recv_sems.at[i], device_id=dev, device_id_type=MESH
-        )
-        copy.start()
-        self.sent.append(copy)
-
-    def arrive(self, key, ref):
-        i = self._id(key)
-        pltpu.make_async_remote_copy(
-            src_ref=ref, dst_ref=ref, send_sem=self.send_sems.at[i], recv_sem=self.recv_sems.at[i], device_id=self.some_peer, device_id_type=MESH
-        ).wait_recv()
-
-    def finish(self):
-        for copy in self.sent:
-            copy.wait_send()
+        kind = key[0]
+        group = kind[:2] if kind[0] == "w" else "h" if kind[0] in "hf" else "x" if kind[0] in "xe" else kind[0]
+        self._copy(group, arrival(key), src, dst, dev).start()
+
+    def arrive(self, arr, ref):
+        self._copy("w1", arr, ref, ref, self.some_peer).wait_recv()
+
+    def finish(self, group, ref):
+        self._copy(group, ("y",), ref, ref, self.some_peer).wait_send()
 
 
 def kernel(nx, ny, x_ref, gamma_ref, w1_ref, w2_ref, out_ref, xland, zb, w1b, w2b, hb, y0, yr, y1, gb, send_sems, recv_sems, loc_sems):
@@ -51,7 +67,7 @@
     T2 = T // 2
     RH = R2 // 2
     T4 = T // 4
-    pieces = [(n, 0, NC) for n in range(CHUNKS - 1)] + [(CHUNKS - 1, 0, NC // 2), (CHUNKS - 1, NC // 2, NC // 2)]
+    pieces = [(0, 0, NC), (0, NC, NC), (1, 0, NC), (1, NC, NC // 2), (1, NC + NC // 2, NC // 2)]
     wpieces = [(j, 0, FC) for j in range(CHUNKS - 1)] + [(CHUNKS - 1, 0, FC // 2), (CHUNKS - 1, FC // 2, FC // 2)]
     NP = len(pieces)
     seq = [(h, j) for h in (0, 1) for j in range(CHUNKS)]
@@ -74,9 +90,11 @@
     local = {}
 
     def local_copy(key, src, dst):
-        copy = pltpu.make_async_copy(src, dst, loc_sems.at[len(local)])
+        copy = pltpu.make_async_copy(src, dst, loc_sems.at[local.setdefault(key, len(local))])
         copy.start()
-        local[key] = copy
+
+    def local_wait(key, ref):
+        pltpu.make_async_copy(ref, ref, loc_sems.at[local[key]]).wait()
 
     def tok(half):
         return pl.ds(half * T2, T2)
@@ -93,7 +111,7 @@
 
     def w2_src(grp, p):
         n, lo, size = pieces[p]
-        return w2_ref.at[pl.ds(pl.multiple_of(grp * RH, RH), RH), pl.ds(n * NC + lo, size)]
+        return w2_ref.at[pl.ds(pl.multiple_of(grp * RH, RH), RH), pl.ds(2 * n * NC + lo, size)]
 
     def w2_dst(p, xx, cc):
         n, lo, size = pieces[p]
@@ -137,17 +155,24 @@
         comm.arrive((w + "f", j), dst(j, xf, c))
         comm.send((w + "c", 3, j), dst(j, xf, c), dst(j, xf, c), PC)
 
-    def w_ready(w, dst, j):
-        for i, xx in enumerate((x, xi, xp, xf)):
-            comm.arrive((w + "c", i, j), dst(j, xx, 1 - c))
-        local[(w, j)].wait()
+    def w1_ready(p):
+        j, lo, size = wpieces[p]
+        comm.arrive(("w1c", False, p), w1b.at[j, pl.ds(0, nx * KR), pl.ds(lo, size)])
+        local_wait(("w1", p), w1_dst(p, x, c))
+
+    def w2_ready(p):
+        n, lo, size = pieces[p]
+        comm.arrive(("w2c", False, p), w2b.at[n, pl.ds(0, (nx - 1) * RH), pl.ds(lo, size)])
+        local_wait(("w2", p), w2_dst(p, x, c))
+
+    def w2_far_ready(p):
+        comm.arrive(("w2c", True, p), w2_dst(p, xf, 1 - c))
 
     def x_load(h):
-        local_copy(("z", h, 0), xland.at[0, y] if h == 0 else x_ref, zb.at[y])
-        for i, yy in enumerate((up, dn, far)):
-            local_copy(("z", h, i + 1), xland.at[h, yy], zb.at[yy])
-        for i in range(4):
-            local[("z", h, i)].wait()
+        local_copy(("z", h), xland.at[0, y] if h == 0 else x_ref, zb.at[y])
+        for yy in (up, dn, far):
+            local_copy(("z", h), xland.at[h, yy], zb.at[yy])
+        local_wait(("z", h), zb)
 
     def norm():
         rb = 32
@@ -195,12 +220,12 @@
         comm.send(("fM", k), hs(k, up, 1), hs(k, up, 1), YM)
 
     def h_ready(k):
-        comm.arrive(("hP", k, 1), hs(k, dn, 1))
-        comm.arrive(("hM", k, 0), hs(k, up, 0))
+        h, j = seq[k]
+        comm.arrive(("h", k), hb.at[h, 0, :, pl.ds(j * FC, FC)])
 
     def far_ready(k):
-        comm.arrive(("fP", k), hs(k, far, 0))
-        comm.arrive(("fM", k), hs(k, far, 1))
+        h, j = seq[k]
+        comm.arrive(("f", k), hb.at[h, 0, :, pl.ds(j * FC, FC)])
 
     def project(h, acc, n, yys, j0, j1, first, cols=slice(None)):
         for yy in yys:
@@ -215,16 +240,9 @@
             else:
                 acc[n, :, cols] += d
 
-    def partial_out(p):
-        n, c0, size = pieces[p]
-        cols = slice(c0, c0 + size)
-        for i, xx in enumerate((x, xi, xp)):
-            comm.arrive(("w2c", i, p), w2_dst(p, xx, 1 - c))
-        local[("w2", p)].wait()
-        project(0, y0, n, (x, xi, xp), 0, CHUNKS, True, cols)
-        comm.arrive(("w2c", 3, p), w2_dst(p, xf, 1 - c))
-        project(0, y0, n, (xf,), 0, CHUNKS, False, cols)
-        comm.send(("y", p), y0.at[n, :, pl.ds(c0, size)], yr.at[n, :, pl.ds(c0, size)], PX)
+    def partial_send(p):
+        n, lo, size = pieces[p]
+        comm.send(("y", p), y0.at[n, :, pl.ds(lo, size)], yr.at[n, :, pl.ds(lo, size)], PX)
 
     def x_relay(quarter):
         comm.arrive(("xp", quarter), xq(0, y, quarter))
@@ -269,26 +287,20 @@
     w1_inner(4)
     w_from_inner("w1", w1_dst, 3)
 
-    local["g"].wait()
-    for yk, yy in (("P", dn), ("M", up), ("F", far)):
-        comm.arrive(("g" + yk,), gb.at[yy])
-    for quarter in (2, 3):
-        comm.arrive(("x0P", quarter), xq(0, dn, quarter))
-        comm.arrive(("x0m", quarter), xq(0, far, quarter))
-    for quarter in (0, 1):
-        comm.arrive(("x0M", quarter), xq(0, up, quarter))
-        comm.arrive(("x0p", quarter), xq(0, far, quarter))
+    local_wait("g", gb.at[y])
+    comm.arrive(("g",), gb.at[pl.ds(0, ny - 1)])
+    comm.arrive(("x0",), xland.at[0, pl.ds(0, 2)])
     x_load(0)
     norm()
     w_from_far("w1", w1_dst, 0)
-    w_ready("w1", w1_dst, 0)
+    w1_ready(0)
     hidden(0)
     for p in range(NP):
         comm.send(("w2c", 0, p), w2_src(g, p), w2_dst(p, x, c), PC)
         local_copy(("w2", p), w2_src(g, p), w2_dst(p, x, c))
     w_from_pair("w1", w1_dst, 2)
     w_from_far("w1", w1_dst, 1)
-    w_ready("w1", w1_dst, 1)
+    w1_ready(1)
     hidden(1)
     relay(0)
     w_from_pair("w1", w1_dst, 3)
@@ -297,19 +309,16 @@
     w2_inner(0)
     w2_inner(1)
     w_from_far("w1", w1_dst, 2)
-    w_ready("w1", w1_dst, 2)
+    w1_ready(2)
     hidden(2)
     relay(1)
     w_from_far("w1", w1_dst, 3)
     w_from_far("w1", w1_dst, 4)
-    w_ready("w1", w1_dst, 3)
-    w_ready("w1", w1_dst, 4)
+    w1_ready(3)
+    w1_ready(4)
     hidden(3)
     relay(2)
-    comm.arrive(("eP",), xl(1, dn, 0))
-    comm.arrive(("eM",), xl(1, up, 1))
-    comm.arrive(("x1p",), xl(1, far, 1))
-    comm.arrive(("x1m",), xl(1, far, 0))
+    comm.arrive(("x1",), xland.at[1, pl.ds(0, 2)])
     x_load(1)
     norm()
     hidden(4)
@@ -320,10 +329,10 @@
     hidden(5)
     w_from_pair("w2", w2_dst, 2)
     w2_inner(3)
+    w2_inner(4)
     w_from_inner("w2", w2_dst, 0)
     w_from_far("w2", w2_dst, 0)
     w_from_pair("w2", w2_dst, 3)
-    w2_inner(4)
     relay(4)
     w_from_pair("w2", w2_dst, 4)
     hidden(6)
@@ -332,53 +341,67 @@
     for k in range(4):
         h_ready(k)
         far_ready(k)
-    partial_out(0)
-    partial_out(1)
+    for p in (0, 1):
+        w2_ready(p)
+        w2_far_ready(p)
+    project(0, y0, 0, range(ny), 0, CHUNKS, True)
+    partial_send(0)
+    partial_send(1)
+    w_from_inner("w2", w2_dst, 2)
     relay(5)
     hidden(7)
     local_copy("xres", x_ref, zb.at[0])
     h_ready(4)
     far_ready(4)
-    for n in (0, 1):
-        project(1, y1, n, range(ny), 0, 1, True)
-    w_from_inner("w2", w2_dst, 2)
+    project(1, y1, 0, range(ny), 0, 1, True)
     w_from_far("w2", w2_dst, 2)
-    partial_out(2)
+    w2_ready(2)
+    project(0, y0, 1, (x, xi, xp), 0, CHUNKS, True, slice(0, NC))
+    w2_far_ready(2)
+    project(0, y0, 1, (xf,), 0, CHUNKS, False, slice(0, NC))
+    partial_send(2)
     relay(6)
-    project(1, y1, 2, range(ny), 0, 1, True)
+    w_from_inner("w2", w2_dst, 3)
+    w_from_inner("w2", w2_dst, 4)
     h_ready(5)
     far_ready(5)
-    w_from_inner("w2", w2_dst, 3)
-    w_from_far("w2", w2_dst, 3)
-    partial_out(3)
-    for n in (0, 1, 2):
-        project(1, y1, n, range(ny), 1, 2, False)
-    w_from_inner("w2", w2_dst, 4)
-    relay(7)
-    w_from_far("w2", w2_dst, 4)
-    partial_out(4)
-    project(1, y1, 3, range(ny), 0, 2, True)
+    project(1, y1, 0, range(ny), 1, 2, False)
+    w2_ready(3)
+    w2_ready(4)
+    project(0, y0, 1, (x, xi, xp), 0, CHUNKS, True, slice(NC, 2 * NC))
+    for p in (3, 4):
+        if p == 4:
+            relay(7)
+        w_from_far("w2", w2_dst, p)
+        w2_far_ready(p)
+        n, lo, size = pieces[p]
+        project(0, y0, 1, (xf,), 0, CHUNKS, False, slice(lo, lo + size))
+        partial_send(p)
+    project(1, y1, 1, range(ny), 0, 2, True)
     h_ready(6)
     far_ready(6)
-    for n in range(CHUNKS):
+    for n in (0, 1):
         project(1, y1, n, range(ny), 2, 3, False)
     h_ready(7)
-    for n in range(CHUNKS):
+    for n in (0, 1):
         project(1, y1, n, (y, up, dn), 3, 4, False)
-    local["xres"].wait()
-    for p in range(NP):
-        n, c0, size = pieces[p]
-        comm.arrive(("y", p), yr.at[n, :, pl.ds(c0, size)])
+    local_wait("xres", zb.at[0])
+    comm.arrive(("y",), yr)
     far_ready(7)
-    for n in range(CHUNKS):
+    for n in (0, 1):
         project(1, y1, n, (far,), 3, 4, False)
-        cols = slice(n * NC, (n + 1) * NC)
+        lo, size = 2 * n * NC, 2 * NC
+        cols = slice(lo, lo + size)
         zb[1, :, cols] = (zb[0, :, cols].astype(jnp.float32) + (y1[n] + yr[n])).astype(jnp.bfloat16)
-        local_copy(("out", n), zb.at[1, :, pl.ds(n * NC, NC)], out_ref.at[:, pl.ds(n * NC, NC)])
-    for n in range(CHUNKS):
-        local[("out", n)].wait()
-    comm.finish()
-    assert len(comm.ids) <= N_SEMS and len(local) <= 32
+        local_copy("out", zb.at[1, :, pl.ds(lo, size)], out_ref.at[:, pl.ds(lo, size)])
+    local_wait("out", out_ref)
+    comm.finish("x", xland.at[:, :, pl.ds(0, T * 7 // 8), :])
+    comm.finish("w1", w1b.at[:, pl.ds(0, (2 * nx - 1) * KR), :])
+    comm.finish("w2", w2b.at[:, pl.ds(0, (2 * nx - 1) * RH), :])
+    comm.finish("h", hb.at[:, pl.ds(0, ny - 1)])
+    comm.finish("y", y0)
+    comm.finish("g", gb.at[pl.ds(0, ny - 1)])
+    assert len(comm.recv_ids) == N_RECV and len(comm.send_ids) == N_SEND and len(local) == N_LOCAL, (len(comm.recv_ids), len(comm.send_ids), len(local))
 
 
 def solution(mesh):
@@ -403,15 +426,15 @@
             scratch_shapes=[
                 pltpu.VMEM((ny, T, D), bf16),
                 pltpu.VMEM((CHUNKS, 2 * nx * KR, FL // 2 // CHUNKS), bf16),
-                pltpu.VMEM((CHUNKS, nx * R2, NC), bf16),
+                pltpu.VMEM((2, nx * R2, 2 * NC), bf16),
                 pltpu.VMEM((2, ny, T, FL // 2), bf16),
-                pltpu.VMEM((CHUNKS, T, NC), f32),
-                pltpu.VMEM((CHUNKS, T, NC), f32),
-                pltpu.VMEM((CHUNKS, T, NC), f32),
+                pltpu.VMEM((2, T, 2 * NC), f32),
+                pltpu.VMEM((2, T, 2 * NC), f32),
+                pltpu.VMEM((2, T, 2 * NC), f32),
                 pltpu.VMEM((ny, 1, D), f32),
-                pltpu.SemaphoreType.DMA((N_SEMS,)),
-                pltpu.SemaphoreType.DMA((N_SEMS,)),
-                pltpu.SemaphoreType.DMA((32,)),
+                pltpu.SemaphoreType.DMA((N_SEND,)),
+                pltpu.SemaphoreType.DMA((N_RECV,)),
+                pltpu.SemaphoreType.DMA((N_LOCAL,)),
             ],
             compiler_params=pltpu.CompilerParams(collective_id=0, has_side_effects=True, vmem_limit_bytes=67043328),
             cost_estimate=pl.CostEstimate(flops=flops, bytes_accessed=64 * T * D, transcendentals=T * FL),

time: 213 us -> 208 us (0.977)
  Pallas kernels: 210 us -> 205 us
    pallas_call x1, Pallas kernels: 210 us -> 205 us  [per_device(): pl.pallas_call(functools.partial(kernel, nx, ny), out_shape=(jax.ShapeDty...]
where the time goes in v4:
time: 208 us
  Pallas kernels  205 us (99%)
  local copies, waits for them, and re-layouts  2.26 us (1%)
    pallas_call x1, Pallas kernels, per_device(): pl.pallas_call(functools.partial(kernel, nx, ny), out_shape=(jax.ShapeDty...  205 us

profile of v4, /device:TPU:97, one launch (start us, length us, event | category | flops | bytes accessed | tf_op | source)
XLA Modules:
  0.0 207.6 jit_solution(1198467097038550004)
XLA Ops:
  0.0 205.3 %ln_mlp.1 = (bf16[512,1024]{1,0:T(8,128)(2,1)}, bf16[2,4,512,1024]{3,2,1,0:T(8,128)(2,1)}) custom-call(bf16[512,1024]{1,0:T(8,128)(2,1)} %bitcast.4, f32[1,1024]{1,0:T(1,128)} %bitcast.5, bf16[512,4096]{1,0:T(8,128)(2,1)} %w1_ref.1, bf16[2048,1024]{1,0:T(8,128)(2,1)} %w2_ref.1), custom_call_target="tpu_custom_call" | custom-call | flops 34359738368 | bytes 33554432 | tf_op jit(solution)/shard_map/ln_mlp/pallas_call | solution.py:421
  205.3 2.3 %copy.6 = bf16[2,256,1024]{2,1,0:T(8,128)(2,1)} copy(bf16[2,256,1024]{2,1,0:T(8,128)(2,1)} %bitcast.3) | data formatting | bytes 2097152

commit v5 on v4

--- a/solution.py
+++ b/solution.py
@@ -10,7 +10,7 @@
 LN_EPS = 1e-5
 MESH = pl.DeviceIdType.MESH
 CHUNKS = 4
-N_RECV, N_SEND, N_LOCAL = 91, 6, 15
+N_RECV, N_SEND, N_LOCAL = 96, 6, 17
 GELU_C = 0.7978845608028654
 
 
@@ -20,8 +20,10 @@
         return ("g",)
     if kind in ("w1c", "w2c"):
         return (kind, key[1] == 3 and kind == "w2c", key[2])
-    if (kind == "x0P" and key[1] >= 2) or (kind == "x0M" and key[1] < 2) or kind in ("x0p", "x0m"):
+    if (kind == "x0P" and key[1] >= 2) or (kind == "x0M" and key[1] < 2):
         return ("x0",)
+    if kind in ("x0p", "x0m"):
+        return ("x0f",)
     if kind in ("x1p", "x1m", "eP", "eM"):
         return ("x1",)
     if (kind == "hP" and key[2] == 1) or (kind == "hM" and key[2] == 0):
@@ -68,8 +70,8 @@
     RH = R2 // 2
     T4 = T // 4
     pieces = [(0, 0, NC), (0, NC, NC), (1, 0, NC), (1, NC, NC // 2), (1, NC + NC // 2, NC // 2)]
-    wpieces = [(j, 0, FC) for j in range(CHUNKS - 1)] + [(CHUNKS - 1, 0, FC // 2), (CHUNKS - 1, FC // 2, FC // 2)]
-    NP = len(pieces)
+    wpieces = [(0, 0, FC // 2), (0, FC // 2, FC // 2), (1, 0, FC), (2, 0, FC), (3, 0, FC // 2), (3, FC // 2, FC // 2)]
+    NP, NW = len(pieces), len(wpieces)
     seq = [(h, j) for h in (0, 1) for j in range(CHUNKS)]
 
     row, y = lax.axis_index("row"), lax.axis_index("col")
@@ -120,6 +122,9 @@
     def xl(h, yy, half):
         return xland.at[h, yy, tok(half), :]
 
+    def xl_all(h):
+        return xland.at[h, 0]
+
     def xq(h, yy, quarter):
         return xland.at[h, yy, pl.ds(quarter * T4, T4), :]
 
@@ -137,9 +142,9 @@
         comm.send(("xp", quarter), x_ref.at[pl.ds(quarter * T4, T4), :], xq(0, y, quarter), PX)
     comm.send(("x1P",), x_ref.at[tok(1), :], xl(1, y, 1), YP)
     comm.send(("x1M",), x_ref.at[tok(0), :], xl(1, y, 0), YM)
-    for p in (0, 1, 2, 3):
+    for p in range(4):
         w1_inner(p)
-    for p in range(NP):
+    for p in range(NW):
         comm.send(("w1x", p), w1_src(1 - g, p), w1_dst(p, x, c), PX)
 
     def w_from_inner(w, dst, j):
@@ -168,11 +173,12 @@
     def w2_far_ready(p):
         comm.arrive(("w2c", True, p), w2_dst(p, xf, 1 - c))
 
-    def x_load(h):
-        local_copy(("z", h), xland.at[0, y] if h == 0 else x_ref, zb.at[y])
-        for yy in (up, dn, far):
-            local_copy(("z", h), xland.at[h, yy], zb.at[yy])
-        local_wait(("z", h), zb)
+    def x_load(key, h, blocks):
+        for yy in blocks:
+            local_copy(("z", h, key), xland.at[h, yy], zb.at[yy])
+
+    def x_loaded(key, h, count):
+        local_wait(("z", h, key), zb.at[pl.ds(0, count)])
 
     def norm():
         rb = 32
@@ -195,23 +201,35 @@
 
         lax.fori_loop(0, T // rb, body, 0)
 
+    def hidden_part(j, rows, blocks):
+        u = None
+        for yy in blocks:
+            base = yy * D
+            if not isinstance(base, int):
+                base = pl.multiple_of(base, D)
+            d = jnp.dot(zb[yy, rows, :], w1b[j, pl.ds(base, D), :], preferred_element_type=jnp.float32)
+            u = d if u is None else u + d
+        return u
+
+    def hidden_store(h, j, rows, u):
+        cdf = 0.5 * (1.0 + jnp.tanh(GELU_C * (u + 0.044715 * (u * u * u))))
+        hb[h, y, rows, j * FC : (j + 1) * FC] = (u * cdf).astype(jnp.bfloat16)
+
+    def hidden_send(k, a, b):
+        comm.send(("hP", k, a), hs(k, y, a), hs(k, y, a), YP)
+        comm.send(("hM", k, b), hs(k, y, b), hs(k, y, b), YM)
+
     def hidden(k):
         h, j = seq[k]
-        mb = T2
 
         def body(i, carry):
-            rows = pl.ds(pl.multiple_of(i * mb, mb), mb)
-            u = jnp.zeros((mb, FC), jnp.float32)
-            for yy in range(ny):
-                u += jnp.dot(zb[yy, rows, :], w1b[j, yy * D : (yy + 1) * D, :], preferred_element_type=jnp.float32)
-            cdf = 0.5 * (1.0 + jnp.tanh(GELU_C * (u + 0.044715 * (u * u * u))))
-            hb[h, y, rows, j * FC : (j + 1) * FC] = (u * cdf).astype(jnp.bfloat16)
+            rows = pl.ds(pl.multiple_of(i * T2, T2), T2)
+            hidden_store(h, j, rows, hidden_part(j, rows, range(ny)))
             return carry
 
-        lax.fori_loop(0, T // mb, body, 0)
-        for a, b in ((0, 1), (1, 0)):
-            comm.send(("hP", k, a), hs(k, y, a), hs(k, y, a), YP)
-            comm.send(("hM", k, b), hs(k, y, b), hs(k, y, b), YM)
+        lax.fori_loop(0, 2, body, 0)
+        hidden_send(k, 0, 1)
+        hidden_send(k, 1, 0)
 
     def relay(k):
         comm.arrive(("hP", k, 0), hs(k, dn, 0))
@@ -227,22 +245,38 @@
         h, j = seq[k]
         comm.arrive(("f", k), hb.at[h, 0, :, pl.ds(j * FC, FC)])
 
-    def project(h, acc, n, yys, j0, j1, first, cols=slice(None)):
-        for yy in yys:
-            lo, depth = j0 * FC, (j1 - j0) * FC
-            base = yy * FH + lo
-            if not isinstance(base, int):
-                base = pl.multiple_of(base, FC)
-            d = jnp.dot(hb[h, yy, :, lo : lo + depth], w2b[n, pl.ds(base, depth), cols], preferred_element_type=jnp.float32)
-            if first:
-                acc[n, :, cols] = d
-                first = False
-            else:
-                acc[n, :, cols] += d
+    def project(h, acc, n, start, count, j0, j1, cols=slice(None), first=False):
+        lo, depth = j0 * FC, (j1 - j0) * FC
+
+        def body(i, carry):
+            rows = pl.ds(pl.multiple_of(i * T2, T2), T2)
+            total = None
+            for b in range(count):
+                yy = (start + b) % ny
+                base = yy * FH + lo
+                if not isinstance(base, int):
+                    base = pl.multiple_of(base, FC)
+                d = jnp.dot(hb[h, yy, rows, lo : lo + depth], w2b[n, pl.ds(base, depth), cols], preferred_element_type=jnp.float32)
+                total = d if total is None else total + d
+            acc[n, rows, cols] = total if first else acc[n, rows, cols] + total
+            return carry
+
+        lax.fori_loop(0, 2, body, 0)
 
     def partial_send(p):
         n, lo, size = pieces[p]
         comm.send(("y", p), y0.at[n, :, pl.ds(lo, size)], yr.at[n, :, pl.ds(lo, size)], PX)
+
+    def early(p):
+        n, lo, size = pieces[p]
+        w2_ready(p)
+        project(0, y0, n, xf + 1, ny - 1, 0, CHUNKS, slice(lo, lo + size), first=True)
+
+    def late(p):
+        n, lo, size = pieces[p]
+        w2_far_ready(p)
+        project(0, y0, n, xf, 1, 0, CHUNKS, slice(lo, lo + size))
+        partial_send(p)
 
     def x_relay(quarter):
         comm.arrive(("xp", quarter), xq(0, y, quarter))
@@ -262,7 +296,7 @@
         comm.send(("g" + yk,), gamma_ref, gb.at[y], dev)
     local_copy("g", gamma_ref, gb.at[y])
     x_relay(2)
-    for p in range(NP):
+    for p in range(NW):
         comm.send(("w1c", 0, p), w1_src(g, p), w1_dst(p, x, c), PC)
         local_copy(("w1", p), w1_src(g, p), w1_dst(p, x, c))
     x_up(0)
@@ -271,55 +305,66 @@
     x_relay(3)
     w_from_inner("w1", w1_dst, 0)
     w_from_inner("w1", w1_dst, 1)
+    w_from_pair("w1", w1_dst, 0)
     x_up(1)
     comm.send(("eP",), xl(0, dn, 0), xl(1, dn, 0), PX)
     comm.arrive(("x1P",), xl(1, dn, 1))
     comm.send(("x1p",), xl(1, dn, 1), xl(1, dn, 1), YP)
+    w_from_pair("w1", w1_dst, 1)
+    w1_inner(4)
     x_down(3)
     comm.send(("eM",), xl(0, up, 1), xl(1, up, 1), PX)
     comm.arrive(("x1M",), xl(1, up, 0))
     comm.send(("x1m",), xl(1, up, 0), xl(1, up, 0), YM)
-    w_from_pair("w1", w1_dst, 0)
     for p in range(NP):
         comm.send(("w2x", p), w2_src(1 - g, p), w2_dst(p, x, c), PX)
     w_from_inner("w1", w1_dst, 2)
-    w_from_pair("w1", w1_dst, 1)
-    w1_inner(4)
     w_from_inner("w1", w1_dst, 3)
+    w_from_far("w1", w1_dst, 0)
+    w_from_pair("w1", w1_dst, 2)
+    w_from_far("w1", w1_dst, 1)
 
     local_wait("g", gb.at[y])
     comm.arrive(("g",), gb.at[pl.ds(0, ny - 1)])
-    comm.arrive(("x0",), xland.at[0, pl.ds(0, 2)])
-    x_load(0)
+    comm.arrive(("x0",), xl_all(0))
+    x_load("near", 0, (y, up, dn))
+    comm.arrive(("x0f",), xl_all(0))
+    x_load("far", 0, (far,))
+    x_loaded("near", 0, ny - 1)
+    x_loaded("far", 0, 1)
     norm()
-    w_from_far("w1", w1_dst, 0)
     w1_ready(0)
+    w1_ready(1)
     hidden(0)
     for p in range(NP):
         comm.send(("w2c", 0, p), w2_src(g, p), w2_dst(p, x, c), PC)
         local_copy(("w2", p), w2_src(g, p), w2_dst(p, x, c))
-    w_from_pair("w1", w1_dst, 2)
-    w_from_far("w1", w1_dst, 1)
-    w1_ready(1)
+    w_from_pair("w1", w1_dst, 3)
+    w1_inner(5)
+    w_from_inner("w1", w1_dst, 4)
+    w_from_far("w1", w1_dst, 2)
+    relay(0)
+    w1_ready(2)
     hidden(1)
-    relay(0)
-    w_from_pair("w1", w1_dst, 3)
-    w_from_inner("w1", w1_dst, 4)
     w_from_pair("w1", w1_dst, 4)
+    w_from_pair("w1", w1_dst, 5)
     w2_inner(0)
     w2_inner(1)
-    w_from_far("w1", w1_dst, 2)
-    w1_ready(2)
+    w_from_far("w1", w1_dst, 3)
+    w1_ready(3)
     hidden(2)
+    w_from_inner("w1", w1_dst, 5)
     relay(1)
-    w_from_far("w1", w1_dst, 3)
     w_from_far("w1", w1_dst, 4)
-    w1_ready(3)
+    w_from_far("w1", w1_dst, 5)
     w1_ready(4)
+    w1_ready(5)
     hidden(3)
     relay(2)
     comm.arrive(("x1",), xland.at[1, pl.ds(0, 2)])
-    x_load(1)
+    local_copy(("z", 1, "near"), x_ref, zb.at[y])
+    x_load("near", 1, (up, dn, far))
+    x_loaded("near", 1, ny)
     norm()
     hidden(4)
     w_from_pair("w2", w2_dst, 0)
@@ -329,71 +374,73 @@
     hidden(5)
     w_from_pair("w2", w2_dst, 2)
     w2_inner(3)
-    w2_inner(4)
     w_from_inner("w2", w2_dst, 0)
     w_from_far("w2", w2_dst, 0)
     w_from_pair("w2", w2_dst, 3)
+    w2_inner(4)
     relay(4)
     w_from_pair("w2", w2_dst, 4)
-    hidden(6)
     w_from_inner("w2", w2_dst, 1)
-    w_from_far("w2", w2_dst, 1)
     for k in range(4):
         h_ready(k)
+    for k in range(3):
         far_ready(k)
-    for p in (0, 1):
-        w2_ready(p)
-        w2_far_ready(p)
-    project(0, y0, 0, range(ny), 0, CHUNKS, True)
+    w2_ready(0)
+    w2_far_ready(0)
+    w_from_far("w2", w2_dst, 1)
+    w2_ready(1)
+    w2_far_ready(1)
+    project(0, y0, 0, dn, ny - 1, 0, CHUNKS, first=True)
+    project(0, y0, 0, far, 1, 0, CHUNKS - 1)
+    far_ready(3)
+    project(0, y0, 0, far, 1, CHUNKS - 1, CHUNKS)
     partial_send(0)
     partial_send(1)
+    hidden(6)
     w_from_inner("w2", w2_dst, 2)
     relay(5)
     hidden(7)
     local_copy("xres", x_ref, zb.at[0])
     h_ready(4)
     far_ready(4)
-    project(1, y1, 0, range(ny), 0, 1, True)
+    project(1, y1, 0, 0, ny, 0, 1, first=True)
     w_from_far("w2", w2_dst, 2)
-    w2_ready(2)
-    project(0, y0, 1, (x, xi, xp), 0, CHUNKS, True, slice(0, NC))
-    w2_far_ready(2)
-    project(0, y0, 1, (xf,), 0, CHUNKS, False, slice(0, NC))
-    partial_send(2)
+    early(2)
+    late(2)
+    w_from_inner("w2", w2_dst, 3)
     relay(6)
-    w_from_inner("w2", w2_dst, 3)
-    w_from_inner("w2", w2_dst, 4)
+    early(3)
+    w_from_far("w2", w2_dst, 3)
+    late(3)
     h_ready(5)
     far_ready(5)
-    project(1, y1, 0, range(ny), 1, 2, False)
-    w2_ready(3)
-    w2_ready(4)
-    project(0, y0, 1, (x, xi, xp), 0, CHUNKS, True, slice(NC, 2 * NC))
-    for p in (3, 4):
-        if p == 4:
-            relay(7)
-        w_from_far("w2", w2_dst, p)
-        w2_far_ready(p)
-        n, lo, size = pieces[p]
-        project(0, y0, 1, (xf,), 0, CHUNKS, False, slice(lo, lo + size))
-        partial_send(p)
-    project(1, y1, 1, range(ny), 0, 2, True)
+    project(1, y1, 0, 0, ny, 1, 2)
+    w_from_inner("w2", w2_dst, 4)
+    early(4)
+    relay(7)
+    w_from_far("w2", w2_dst, 4)
+    late(4)
+    project(1, y1, 1, 0, ny, 0, 2, first=True)
     h_ready(6)
+    h_ready(7)
+    for n in (0, 1):
+        project(1, y1, n, dn, ny - 1, 2, 4)
     far_ready(6)
     for n in (0, 1):
-        project(1, y1, n, range(ny), 2, 3, False)
-    h_ready(7)
-    for n in (0, 1):
-        project(1, y1, n, (y, up, dn), 3, 4, False)
+        project(1, y1, n, far, 1, 2, 3)
     local_wait("xres", zb.at[0])
     comm.arrive(("y",), yr)
+    for n in (0, 1):
+        y1[n] = y1[n] + yr[n] + zb[0, :, 2 * n * NC : 2 * (n + 1) * NC].astype(jnp.float32)
     far_ready(7)
     for n in (0, 1):
-        project(1, y1, n, (far,), 3, 4, False)
-        lo, size = 2 * n * NC, 2 * NC
-        cols = slice(lo, lo + size)
-        zb[1, :, cols] = (zb[0, :, cols].astype(jnp.float32) + (y1[n] + yr[n])).astype(jnp.bfloat16)
-        local_copy("out", zb.at[1, :, pl.ds(lo, size)], out_ref.at[:, pl.ds(lo, size)])
+        cols = pl.ds(2 * n * NC, 2 * NC)
+        base = pl.multiple_of(far * FH + 3 * FC, FC)
+        for half in (0, 1):
+            rows = slice(half * T2, (half + 1) * T2)
+            last = jnp.dot(hb[1, far, rows, 3 * FC :], w2b[n, pl.ds(base, FC), :], preferred_element_type=jnp.float32)
+            zb[1, rows, 2 * n * NC : 2 * (n + 1) * NC] = (y1[n, rows, :] + last).astype(jnp.bfloat16)
+            local_copy("out", zb.at[1, tok(half), cols], out_ref.at[tok(half), cols])
     local_wait("out", out_ref)
     comm.finish("x", xland.at[:, :, pl.ds(0, T * 7 // 8), :])
     comm.finish("w1", w1b.at[:, pl.ds(0, (2 * nx - 1) * KR), :])

time: 208 us -> 205 us (0.986)
    pallas_call x1, Pallas kernels: 205 us -> 203 us  [per_device(): pl.pallas_call(functools.partial(kernel, nx, ny), out_shape=(jax.ShapeDty...]
where the time goes in v5:
time: 205 us
  Pallas kernels  203 us (99%)
  local copies, waits for them, and re-layouts  2.26 us (1%)
    pallas_call x1, Pallas kernels, per_device(): pl.pallas_call(functools.partial(kernel, nx, ny), out_shape=(jax.ShapeDty...  203 us

profile of v5, /device:TPU:97, one launch (start us, length us, event | category | flops | bytes accessed | tf_op | source)
XLA Modules:
  0.0 204.9 jit_solution(4610571405888220134)
XLA Ops:
  0.0 202.6 %ln_mlp.1 = (bf16[512,1024]{1,0:T(8,128)(2,1)}, bf16[2,4,512,1024]{3,2,1,0:T(8,128)(2,1)}) custom-call(bf16[512,1024]{1,0:T(8,128)(2,1)} %bitcast.4, f32[1,1024]{1,0:T(1,128)} %bitcast.5, bf16[512,4096]{1,0:T(8,128)(2,1)} %w1_ref.1, bf16[2048,1024]{1,0:T(8,128)(2,1)} %w2_ref.1), custom_call_target="tpu_custom_call" | custom-call | flops 34359738368 | bytes 33554432 | tf_op jit(solution)/shard_map/ln_mlp/pallas_call | solution.py:468
  202.6 2.3 %copy.6 = bf16[2,256,1024]{2,1,0:T(8,128)(2,1)} copy(bf16[2,256,1024]{2,1,0:T(8,128)(2,1)} %bitcast.3) | data formatting | bytes 2097152

commit v6 on v5

--- a/solution.py
+++ b/solution.py
@@ -24,7 +24,7 @@
         return ("x0",)
     if kind in ("x0p", "x0m"):
         return ("x0f",)
-    if kind in ("x1p", "x1m", "eP", "eM"):
+    if kind in ("x1p", "x1m", "eP", "eM", "eF"):
         return ("x1",)
     if (kind == "hP" and key[2] == 1) or (kind == "hM" and key[2] == 0):
         return ("h", key[1])
@@ -68,7 +68,7 @@
     NC = N // CHUNKS
     T2 = T // 2
     RH = R2 // 2
-    T4 = T // 4
+    T4, T8 = T // 4, T // 8
     pieces = [(0, 0, NC), (0, NC, NC), (1, 0, NC), (1, NC, NC // 2), (1, NC + NC // 2, NC // 2)]
     wpieces = [(0, 0, FC // 2), (0, FC // 2, FC // 2), (1, 0, FC), (2, 0, FC), (3, 0, FC // 2), (3, FC // 2, FC // 2)]
     NP, NW = len(pieces), len(wpieces)
@@ -121,6 +121,9 @@
 
     def xl(h, yy, half):
         return xland.at[h, yy, tok(half), :]
+
+    def xs(h, yy, first, count):
+        return xland.at[h, yy, pl.ds(first, count), :]
 
     def xl_all(h):
         return xland.at[h, 0]
@@ -227,15 +230,28 @@
             hidden_store(h, j, rows, hidden_part(j, rows, range(ny)))
             return carry
 
-        lax.fori_loop(0, 2, body, 0)
-        hidden_send(k, 0, 1)
-        hidden_send(k, 1, 0)
-
-    def relay(k):
+        if k == 0:
+            body(0, 0)
+            comm.send(("hP", k, 0), hs(k, y, 0), hs(k, y, 0), YP)
+            body(1, 0)
+            comm.send(("hM", k, 1), hs(k, y, 1), hs(k, y, 1), YM)
+            hidden_send(k, 1, 0)
+        else:
+            lax.fori_loop(0, 2, body, 0)
+            hidden_send(k, 0, 1)
+            hidden_send(k, 1, 0)
+
+    def relay_up(k):
         comm.arrive(("hP", k, 0), hs(k, dn, 0))
         comm.send(("fP", k), hs(k, dn, 0), hs(k, dn, 0), YP)
+
+    def relay_down(k):
         comm.arrive(("hM", k, 1), hs(k, up, 1))
         comm.send(("fM", k), hs(k, up, 1), hs(k, up, 1), YM)
+
+    def relay(k):
+        relay_up(k)
+        relay_down(k)
 
     def h_ready(k):
         h, j = seq[k]
@@ -309,15 +325,13 @@
     x_up(1)
     comm.send(("eP",), xl(0, dn, 0), xl(1, dn, 0), PX)
     comm.arrive(("x1P",), xl(1, dn, 1))
-    comm.send(("x1p",), xl(1, dn, 1), xl(1, dn, 1), YP)
+    comm.send(("x1p",), xs(1, dn, T2, T2 - T8), xs(1, dn, T2, T2 - T8), YP)
     w_from_pair("w1", w1_dst, 1)
     w1_inner(4)
     x_down(3)
     comm.send(("eM",), xl(0, up, 1), xl(1, up, 1), PX)
     comm.arrive(("x1M",), xl(1, up, 0))
-    comm.send(("x1m",), xl(1, up, 0), xl(1, up, 0), YM)
-    for p in range(NP):
-        comm.send(("w2x", p), w2_src(1 - g, p), w2_dst(p, x, c), PX)
+    comm.send(("x1m",), xs(1, up, 0, T2 - T8), xs(1, up, 0, T2 - T8), YM)
     w_from_inner("w1", w1_dst, 2)
     w_from_inner("w1", w1_dst, 3)
     w_from_far("w1", w1_dst, 0)
@@ -330,6 +344,10 @@
     x_load("near", 0, (y, up, dn))
     comm.arrive(("x0f",), xl_all(0))
     x_load("far", 0, (far,))
+    for first in (T2 - T8, T - T8):
+        comm.send(("eF", first), xs(0, far, first, T8), xs(1, far, first, T8), PX)
+    for p in range(NP):
+        comm.send(("w2x", p), w2_src(1 - g, p), w2_dst(p, x, c), PX)
     x_loaded("near", 0, ny - 1)
     x_loaded("far", 0, 1)
     norm()
@@ -372,14 +390,11 @@
     w2_inner(2)
     relay(3)
     hidden(5)
+    w_from_inner("w2", w2_dst, 0)
+    w_from_far("w2", w2_dst, 0)
     w_from_pair("w2", w2_dst, 2)
     w2_inner(3)
-    w_from_inner("w2", w2_dst, 0)
-    w_from_far("w2", w2_dst, 0)
-    w_from_pair("w2", w2_dst, 3)
-    w2_inner(4)
     relay(4)
-    w_from_pair("w2", w2_dst, 4)
     w_from_inner("w2", w2_dst, 1)
     for k in range(4):
         h_ready(k)
@@ -396,6 +411,9 @@
     project(0, y0, 0, far, 1, CHUNKS - 1, CHUNKS)
     partial_send(0)
     partial_send(1)
+    w_from_pair("w2", w2_dst, 3)
+    w2_inner(4)
+    w_from_pair("w2", w2_dst, 4)
     hidden(6)
     w_from_inner("w2", w2_dst, 2)
     relay(5)

time: 205 us -> 204 us (level)
  no operation moved by 1% of the time
where the time goes in v6:
time: 204 us; the launch traced here: 203 us
  Pallas kernels  201 us (99%)
  local copies, waits for them, and re-layouts  2.26 us (1%)
    pallas_call x1, Pallas kernels, per_device(): pl.pallas_call(functools.partial(kernel, nx, ny), out_shape=(jax.ShapeDty...  201 us

profile of v6, /device:TPU:97, one launch (start us, length us, event | category | flops | bytes accessed | tf_op | source)
XLA Modules:
  0.0 203.4 jit_solution(2476605667204151146)
XLA Ops:
  0.0 201.1 %ln_mlp.1 = (bf16[512,1024]{1,0:T(8,128)(2,1)}, bf16[2,4,512,1024]{3,2,1,0:T(8,128)(2,1)}) custom-call(bf16[512,1024]{1,0:T(8,128)(2,1)} %bitcast.4, f32[1,1024]{1,0:T(1,128)} %bitcast.5, bf16[512,4096]{1,0:T(8,128)(2,1)} %w1_ref.1, bf16[2048,1024]{1,0:T(8,128)(2,1)} %w2_ref.1), custom_call_target="tpu_custom_call" | custom-call | flops 34359738368 | bytes 33554432 | tf_op jit(solution)/shard_map/ln_mlp/pallas_call | solution.py:486
  201.2 2.3 %copy.6 = bf16[2,256,1024]{2,1,0:T(8,128)(2,1)} copy(bf16[2,256,1024]{2,1,0:T(8,128)(2,1)} %bitcast.3) | data formatting | bytes 2097152
